TPU v7x, 256 devices: a whole 4x4x8 slice. The times are simulated.
256 devices in a mesh: gz: 32 (over y, z), gy: 4 (over x), gx: 2 (over core).
Axes of the slice: x: 4, y: 4, z: 8, core: 2. Of those that a mesh axis runs over, the one named last changes fastest.
Arguments:
- right_side: float32 [256, 64, 256], P('gz', 'gy', 'gx'), may hold values from -128 to 128
- diagonal: float32 [256, 64, 256], P('gz', 'gy', 'gx'), may hold values from 0.05 to 1
Outputs:
- solution_field: float32 [256, 64, 256], P('gz', 'gy', 'gx')
- residual: float32 [256, 64, 256], P('gz', 'gy', 'gx')
All inputs are finite; a program needn't handle non-finite values.
Results may differ from a plain program's by a relative error of at most 0.03.
Values sent between devices are 32-bit elements.
A program may use at most 64 MiB of HBM per device.

v0:
```python
import functools

import jax
import jax.numpy as jnp
import numpy as np
from jax import lax
from jax.sharding import Mesh
from jax.sharding import PartitionSpec as P

S = 6
OUTER = 5
GZ = ("gz_0", "gz_1")


center_shift = 19.0
half_width = 19.0


def extended_2(block, sides, width, periodic):
    for axis, dim in sides:
        count = lax.axis_size(axis)
        forward = [(i, i + 1) for i in range(count - 1)]
        if periodic:
            forward.append((count - 1, 0))
        backward = [(target, source) for source, target in forward]
        low = lax.ppermute(
            lax.slice_in_dim(block, block.shape[dim] - width, None, axis=dim), axis, forward
        )
        high = lax.ppermute(lax.slice_in_dim(block, 0, width, axis=dim), axis, backward)
        block = jnp.concatenate([low, block, high], axis=dim)
    return block


def over_axes(shard, axes):
    return functools.reduce(lax.psum, axes, shard)


def apply_operator(padded, diagonal):
    extent_z = padded.shape[-3] - 2
    extent_y = padded.shape[-2] - 2
    extent_x = padded.shape[-1] - 2
    running = jnp.zeros(padded[..., 1:-1, 1:-1, 1:-1].shape, jnp.float32)
    for along_z in range(3):
        for along_y in range(3):
            for along_x in range(3):
                if along_z == 1 and along_y == 1 and (along_x == 1):
                    continue
                running = (
                    running
                    + padded[
                        ...,
                        along_z : along_z + extent_z,
                        along_y : along_y + extent_y,
                        along_x : along_x + extent_x,
                    ]
                )
    return (26.0 + diagonal) * padded[..., 1:-1, 1:-1, 1:-1] - running


def chebyshev_next(images, current, previous):
    scaled = (images - center_shift * current) / half_width
    if previous is None:
        return scaled
    return 2.0 * scaled - previous


def basis_change():
    columns = 2 * S + 1
    matrix = np.zeros((columns, columns), np.float32)
    for offset, length in ((0, S), (S + 1, S - 1)):
        for degree in range(length):
            matrix[offset + degree, offset + degree] = center_shift
            if degree == 0:
                matrix[offset + 1, offset] = half_width
            else:
                matrix[offset + degree + 1, offset + degree] = 0.5 * half_width
                matrix[offset + degree - 1, offset + degree] = 0.5 * half_width
    return matrix


def coefficients(gram_matrix):
    columns = 2 * S + 1
    change = jnp.asarray(basis_change(), dtype=jnp.float32)
    identity = jnp.eye(columns, dtype=jnp.float32)
    dir_coeff = identity[0]
    res_coeff = identity[S + 1]
    sol_coeff = jnp.zeros((columns,), jnp.float32)
    for degree in range(S):
        moved = jnp.dot(change, dir_coeff, precision=lax.Precision.HIGHEST)
        norm_now = jnp.dot(
            res_coeff,
            jnp.dot(gram_matrix, res_coeff, precision=lax.Precision.HIGHEST),
            precision=lax.Precision.HIGHEST,
        )
        curvature = jnp.dot(
            dir_coeff,
            jnp.dot(gram_matrix, moved, precision=lax.Precision.HIGHEST),
            precision=lax.Precision.HIGHEST,
        )
        step_len = norm_now / curvature
        sol_coeff = sol_coeff + step_len * dir_coeff
        res_next = res_coeff - step_len * moved
        norm_next = jnp.dot(
            res_next,
            jnp.dot(gram_matrix, res_next, precision=lax.Precision.HIGHEST),
            precision=lax.Precision.HIGHEST,
        )
        dir_coeff = res_next + norm_next / norm_now * dir_coeff
        res_coeff = res_next
    return (sol_coeff, res_coeff, dir_coeff)


def combine(coeff, basis_set):
    return jnp.tensordot(coeff, basis_set, axes=1, precision=lax.Precision.HIGHEST)


def crop_margin(values, amount):
    if amount == 0:
        return values
    return values[..., amount:-amount, amount:-amount, amount:-amount]


def band_powers(start_field, margin, count, diagonal_ext, inside):
    fields = [start_field]
    margins = [margin]
    for degree in range(count):
        current = fields[-1]
        out_margin = margins[-1] - 1
        trim = S - out_margin
        images = apply_operator(current, crop_margin(diagonal_ext, trim)) * crop_margin(
            inside, trim
        )
        previous = crop_margin(fields[-2], 2) if degree else None
        fields.append(chebyshev_next(images, crop_margin(current, 1), previous))
        margins.append(out_margin)
    return [crop_margin(one_field, edge_width) for one_field, edge_width in zip(fields, margins)]


def local(right_side, diagonal):
    block_z, block_y, block_x = diagonal.shape
    solution = jnp.zeros(right_side.shape, jnp.float32)
    residual = right_side
    direction = right_side
    diagonal_ext = extended_2(diagonal, ((GZ, 0), ("gy", 1), ("gx", 2)), S, False)
    ext_shape = diagonal_ext.shape
    z_index = lax.broadcasted_iota(jnp.int32, ext_shape, 0) + lax.axis_index(GZ) * block_z - S
    y_index = lax.broadcasted_iota(jnp.int32, ext_shape, 1) + lax.axis_index("gy") * block_y - S
    x_index = lax.broadcasted_iota(jnp.int32, ext_shape, 2) + lax.axis_index("gx") * block_x - S
    inside = (
        (z_index >= 0)
        & (z_index < block_z * lax.axis_size(GZ))
        & (y_index >= 0)
        & (y_index < block_y * lax.axis_size("gy"))
        & (x_index >= 0)
        & (x_index < block_x * lax.axis_size("gx"))
    ).astype(jnp.float32)
    for outer_step in range(OUTER):
        extended = extended_2(
            jnp.stack([direction, residual]), ((GZ, 1), ("gy", 2), ("gx", 3)), S, False
        )
        p_fields = band_powers(extended[0], S, S, diagonal_ext, inside)
        r_fields = band_powers(crop_margin(extended[1], 1), S - 1, S - 1, diagonal_ext, inside)
        basis_set = jnp.stack(p_fields + r_fields)
        flattened = basis_set.reshape(basis_set.shape[0], -1)
        local_gram = jnp.dot(flattened, flattened.T, precision=lax.Precision.HIGHEST)
        partial_gram = over_axes(local_gram, ("gy", "gx"))
        gram_matrix = over_axes(partial_gram, GZ)
        sol_coeff, res_coeff, dir_coeff = coefficients(gram_matrix)
        solution = solution + combine(sol_coeff, basis_set)
        residual = combine(res_coeff, basis_set)
        direction = combine(dir_coeff, basis_set)
    return (solution, residual)


def solution(mesh):
    finer = Mesh(
        mesh.devices.reshape(4, 8, mesh.shape["gy"], mesh.shape["gx"]), ("gz_0", "gz_1", "gy", "gx")
    )
    in_specs = (P(GZ, "gy", "gx"), P(GZ, "gy", "gx"))
    out_specs = (P(GZ, "gy", "gx"), P(GZ, "gy", "gx"))
    return jax.shard_map(local, mesh=finer, in_specs=in_specs, out_specs=out_specs, check_vma=False)
```

profile of v0, /device:TPU:10, one launch (start us, length us, event | category | flops | bytes accessed | tf_op | source)
XLA Modules:
  0.0 646.3 jit_solution(16633903214098267398)
XLA Ops:
  1.6 7.6 %collective-permute-start.7 = (f32[6,16,128]{2,1,0:T(8,128)S(1)}, f32[6,16,128]{2,1,0:T(8,128)S(1)}, u32[]{:S(2)}, u32[]{:S(2)}) collective-permute-start(f32[6,16,128]{2,1,0:T(8,128)S(1)} %get-tuple-element.44), channel_id=1, source_target_pairs={{8,0},{16,8},{24,16},{32,24},{40,32},{48,40},{56,48},{64,56},{72,6... | collective-permute-start | bytes 147464 | tf_op jit(solution)/shard_map/ppermute | solution.py:29
  14.1 6.0 collective-permute-start.1
  21.4 3.4 collective-permute-start.8
  24.8 2.4 collective-permute-start.9
  27.3 3.4 collective-permute-start.2
  30.7 2.4 collective-permute-start.3
  40.9 3.9 collective-permute-start.4
  49.0 3.0 fusion.225
  57.9 3.4 fusion.125
  61.4 2.2 slice_subtract_fusion.4
  72.4 8.7 %psum.140 = f32[13,13]{1,0:T(8,128)S(1)} all-reduce(f32[13,13]{1,0:T(8,128)S(1)} %convolution_bitcast_fusion), channel_id=1, replica_groups=mesh['gz_0'=4,'gz_1'=8,'gy'=4,'gx'=2] {'gy'}, use_global_device_ids=true, to_apply=%region_0.0 | all-reduce | flops 169 | bytes 1352 | tf_op jit(solution)/shard_map/psum | solution.py:35
  81.1 2.5 psum.141
  83.6 8.8 %psum.142 = f32[13,13]{1,0:T(8,128)S(1)} all-reduce(f32[13,13]{1,0:T(8,128)S(1)} %psum.141), channel_id=1, replica_groups=mesh['gz_0'=4,'gz_1'=8,'gy'=4,'gx'=2] {'gz_0'}, use_global_device_ids=true, to_apply=%region_2.0 | all-reduce | flops 169 | bytes 1352 | tf_op jit(solution)/shard_map/psum | solution.py:35
  92.4 16.5 %psum.143 = f32[13,13]{1,0:T(8,128)S(1)} all-reduce(f32[13,13]{1,0:T(8,128)S(1)} %psum.142), channel_id=1, replica_groups=mesh['gz_0'=4,'gz_1'=8,'gy'=4,'gx'=2] {'gz_1'}, use_global_device_ids=true, to_apply=%region_3.0 | all-reduce | flops 169 | bytes 1352 | tf_op jit(solution)/shard_map/psum | solution.py:35
  138.7 6.0 collective-permute-start.13
  147.0 3.3 collective-permute-start.14
  150.3 2.7 collective-permute-start.15
  154.4 3.1 collective-permute-done.15
  159.4 2.1 copy.45
  167.9 2.1 copy.48
  172.1 3.1 fusion.121
  175.3 3.0 fusion.217
  183.4 2.6 slice_subtract_fusion.3
  194.5 8.7 %psum.144 = f32[13,13]{1,0:T(8,128)S(1)} all-reduce(f32[13,13]{1,0:T(8,128)S(1)} %fusion.33), channel_id=1, replica_groups=mesh['gz_0'=4,'gz_1'=8,'gy'=4,'gx'=2] {'gy'}, use_global_device_ids=true, to_apply=%region_4.0 | all-reduce | flops 169 | bytes 1352 | tf_op jit(solution)/shard_map/psum | solution.py:35
  203.1 2.5 psum.145
  205.6 8.8 %psum.146 = f32[13,13]{1,0:T(8,128)S(1)} all-reduce(f32[13,13]{1,0:T(8,128)S(1)} %psum.145), channel_id=1, replica_groups=mesh['gz_0'=4,'gz_1'=8,'gy'=4,'gx'=2] {'gz_0'}, use_global_device_ids=true, to_apply=%region_6.0 | all-reduce | flops 169 | bytes 1352 | tf_op jit(solution)/shard_map/psum | solution.py:35
  214.4 18.5 %psum.147 = f32[13,13]{1,0:T(8,128)S(1)} all-reduce(f32[13,13]{1,0:T(8,128)S(1)} %psum.146), channel_id=1, replica_groups=mesh['gz_0'=4,'gz_1'=8,'gy'=4,'gx'=2] {'gz_1'}, use_global_device_ids=true, to_apply=%region_7.0 | all-reduce | flops 169 | bytes 1352 | tf_op jit(solution)/shard_map/psum | solution.py:35
  263.7 6.0 collective-permute-start.19
  273.9 3.9 collective-permute-start.21
  283.2 2.1 copy.51
  287.2 2.1 copy.52
  290.7 2.1 copy.53
  292.8 2.1 copy.54
  294.9 2.2 pad_maximum_fusion.2
  297.2 3.1 fusion.117
  300.4 3.0 fusion.209
  308.5 2.6 slice_subtract_fusion.2
  320.5 9.8 %psum.148 = f32[13,13]{1,0:T(8,128)S(1)} all-reduce(f32[13,13]{1,0:T(8,128)S(1)} %fusion.36), channel_id=1, replica_groups=mesh['gz_0'=4,'gz_1'=8,'gy'=4,'gx'=2] {'gy'}, use_global_device_ids=true, to_apply=%region_8.0 | all-reduce | flops 169 | bytes 1352 | tf_op jit(solution)/shard_map/psum | solution.py:35
  330.4 2.5 psum.149
  332.9 6.6 %psum.150 = f32[13,13]{1,0:T(8,128)S(1)} all-reduce(f32[13,13]{1,0:T(8,128)S(1)} %psum.149), channel_id=1, replica_groups=mesh['gz_0'=4,'gz_1'=8,'gy'=4,'gx'=2] {'gz_0'}, use_global_device_ids=true, to_apply=%region_10.0 | all-reduce | flops 169 | bytes 1352 | tf_op jit(solution)/shard_map/psum | solution.py:35
  339.5 20.7 %psum.151 = f32[13,13]{1,0:T(8,128)S(1)} all-reduce(f32[13,13]{1,0:T(8,128)S(1)} %psum.150), channel_id=1, replica_groups=mesh['gz_0'=4,'gz_1'=8,'gy'=4,'gx'=2] {'gz_1'}, use_global_device_ids=true, to_apply=%region_11.0 | all-reduce | flops 169 | bytes 1352 | tf_op jit(solution)/shard_map/psum | solution.py:35
  385.4 2.3 fusion.8
  389.0 2.3 fusion.10
  393.3 6.0 collective-permute-start.25
  403.5 3.9 collective-permute-start.27
  416.9 4.5 collective-permute-start.28
  428.0 3.1 fusion.113
  431.2 3.0 fusion.201
  439.6 2.2 slice_subtract_fusion.1
  450.3 9.8 %psum.152 = f32[13,13]{1,0:T(8,128)S(1)} all-reduce(f32[13,13]{1,0:T(8,128)S(1)} %fusion.39), channel_id=1, replica_groups=mesh['gz_0'=4,'gz_1'=8,'gy'=4,'gx'=2] {'gy'}, use_global_device_ids=true, to_apply=%region_12.0 | all-reduce | flops 169 | bytes 1352 | tf_op jit(solution)/shard_map/psum | solution.py:35
  460.2 2.5 psum.153
  462.7 6.6 %psum.154 = f32[13,13]{1,0:T(8,128)S(1)} all-reduce(f32[13,13]{1,0:T(8,128)S(1)} %psum.153), channel_id=1, replica_groups=mesh['gz_0'=4,'gz_1'=8,'gy'=4,'gx'=2] {'gz_0'}, use_global_device_ids=true, to_apply=%region_14.0 | all-reduce | flops 169 | bytes 1352 | tf_op jit(solution)/shard_map/psum | solution.py:35
  469.3 20.7 %psum.155 = f32[13,13]{1,0:T(8,128)S(1)} all-reduce(f32[13,13]{1,0:T(8,128)S(1)} %psum.154), channel_id=1, replica_groups=mesh['gz_0'=4,'gz_1'=8,'gy'=4,'gx'=2] {'gz_1'}, use_global_device_ids=true, to_apply=%region_15.0 | all-reduce | flops 169 | bytes 1352 | tf_op jit(solution)/shard_map/psum | solution.py:35
  521.0 6.0 collective-permute-start.31
  531.2 3.9 collective-permute-start.33
  540.3 2.1 copy.63
  544.0 4.4 collective-permute-start.34
  554.7 3.1 fusion.109
  557.9 3.0 fusion.193
  566.1 2.2 slice_subtract_fusion
  576.9 10.0 %psum.156 = f32[13,13]{1,0:T(8,128)S(1)} all-reduce(f32[13,13]{1,0:T(8,128)S(1)} %fusion.30), channel_id=1, replica_groups=mesh['gz_0'=4,'gz_1'=8,'gy'=4,'gx'=2] {'gy'}, use_global_device_ids=true, to_apply=%region_16.0 | all-reduce | flops 169 | bytes 1352 | tf_op jit(solution)/shard_map/psum | solution.py:35
  586.9 2.5 psum.157
  589.4 6.6 %psum.158 = f32[13,13]{1,0:T(8,128)S(1)} all-reduce(f32[13,13]{1,0:T(8,128)S(1)} %psum.157), channel_id=1, replica_groups=mesh['gz_0'=4,'gz_1'=8,'gy'=4,'gx'=2] {'gz_0'}, use_global_device_ids=true, to_apply=%region_18.0 | all-reduce | flops 169 | bytes 1352 | tf_op jit(solution)/shard_map/psum | solution.py:35
  596.0 20.9 %psum.159 = f32[13,13]{1,0:T(8,128)S(1)} all-reduce(f32[13,13]{1,0:T(8,128)S(1)} %psum.158), channel_id=1, replica_groups=mesh['gz_0'=4,'gz_1'=8,'gy'=4,'gx'=2] {'gz_1'}, use_global_device_ids=true, to_apply=%region_19.0 | all-reduce | flops 169 | bytes 1352 | tf_op jit(solution)/shard_map/psum | solution.py:35
  (502 shorter events, 221.7 us)
Async XLA Ops:
  0.6 20.7 %copy-start.2 = (f32[8,16,128]{2,1,0:T(8,128)S(1)}, f32[8,16,128]{2,1,0:T(8,128)}, u32[]{:S(2)}) copy-start(f32[8,16,128]{2,1,0:T(8,128)} %param.8) | copy-start | bytes 196612
  0.6 26.6 %copy-start.6 = (f32[8,16,128]{2,1,0:T(8,128)S(1)}, f32[8,16,128]{2,1,0:T(8,128)}, u32[]{:S(2)}) copy-start(f32[8,16,128]{2,1,0:T(8,128)} %param.7) | copy-start | bytes 196612
  1.6 19.7 %collective-permute-start.7 = (f32[6,16,128]{2,1,0:T(8,128)S(1)}, f32[6,16,128]{2,1,0:T(8,128)S(1)}, u32[]{:S(2)}, u32[]{:S(2)}) collective-permute-start(f32[6,16,128]{2,1,0:T(8,128)S(1)} %get-tuple-element.44), channel_id=1, source_target_pairs={{8,0},{16,8},{24,16},{32,24},{40,32},{48,40},{56,48},{64,56},{72,6... | collective-permute-start | bytes 147464 | tf_op jit(solution)/shard_map/ppermute | solution.py:29
  9.2 12.0 %collective-permute-start.6 = (f32[6,16,128]{2,1,0:T(8,128)S(1)}, f32[6,16,128]{2,1,0:T(8,128)S(1)}, u32[]{:S(2)}, u32[]{:S(2)}) collective-permute-start(f32[6,16,128]{2,1,0:T(8,128)S(1)} %get-tuple-element.45), channel_id=1, source_target_pairs={{0,8},{8,16},{16,24},{24,32},{32,40},{40,48},{48,56},{56,64},{64,7... | collective-permute-start | bytes 147464 | tf_op jit(solution)/shard_map/ppermute | solution.py:26
  12.1 15.1 %collective-permute-start = (f32[2,6,16,128]{3,2,1,0:T(8,128)S(1)}, f32[2,6,16,128]{3,2,1,0:T(8,128)S(1)}, u32[]{:S(2)}, u32[]{:S(2)}) collective-permute-start(f32[2,6,16,128]{3,2,1,0:T(8,128)S(1)} %get-tuple-element.46), channel_id=1, source_target_pairs={{0,8},{8,16},{16,24},{24,32},{32,40},{40,48},{48,56},{56,64},{64,7... | collective-permute-start | bytes 294920 | tf_op jit(solution)/shard_map/ppermute | solution.py:26
  14.1 13.2 %collective-permute-start.1 = (f32[2,6,16,128]{3,2,1,0:T(8,128)S(1)}, f32[2,6,16,128]{3,2,1,0:T(8,128)S(1)}, u32[]{:S(2)}, u32[]{:S(2)}) collective-permute-start(f32[2,6,16,128]{3,2,1,0:T(8,128)S(1)} %get-tuple-element.47), channel_id=1, source_target_pairs={{8,0},{16,8},{24,16},{32,24},{40,32},{48,40},{56,48},{64,56},{72,6... | collective-permute-start | bytes 294920 | tf_op jit(solution)/shard_map/ppermute | solution.py:29
  20.1 340.8 %copy-start.23 = (pred[13,13]{1,0:T(8,128)(4,1)}, pred[13,13]{1,0:T(8,128)(4,1)S(1)}, u32[]{:S(2)}) copy-start(pred[13,13]{1,0:T(8,128)(4,1)S(1)} %iota_compare_fusion) | copy-start | bytes 511
  21.0 342.0 %copy-start.20 = (f32[1,13]{1,0:T(1,128)}, f32[1,13]{1,0:T(1,128)S(1)}, u32[]{:S(2)}) copy-start(f32[1,13]{1,0:T(1,128)S(1)} %fusion.419) | copy-start | bytes 160
  21.4 11.8 %collective-permute-start.8 = (f32[20,6,128]{2,1,0:T(8,128)S(1)}, f32[20,6,128]{2,1,0:T(8,128)S(1)}, u32[]{:S(2)}, u32[]{:S(2)}) collective-permute-start(f32[20,6,128]{2,1,0:T(8,128)S(1)} %get-tuple-element.34), channel_id=1, source_target_pairs={{0,2},{2,4},{4,6},{1,3},{3,5},{5,7},{8,10},{10,12},{12,14},{9,11},... | collective-permute-start | bytes 184328 | tf_op jit(solution)/shard_map/ppermute | solution.py:26
  24.8 8.4 %collective-permute-start.9 = (f32[20,6,128]{2,1,0:T(8,128)S(1)}, f32[20,6,128]{2,1,0:T(8,128)S(1)}, u32[]{:S(2)}, u32[]{:S(2)}) collective-permute-start(f32[20,6,128]{2,1,0:T(8,128)S(1)} %get-tuple-element.35), channel_id=1, source_target_pairs={{2,0},{4,2},{6,4},{3,1},{5,3},{7,5},{10,8},{12,10},{14,12},{11,9},... | collective-permute-start | bytes 184328 | tf_op jit(solution)/shard_map/ppermute | solution.py:29
  27.3 10.1 %collective-permute-start.2 = (f32[2,20,6,128]{3,2,1,0:T(8,128)S(1)}, f32[2,20,6,128]{3,2,1,0:T(8,128)S(1)}, u32[]{:S(2)}, u32[]{:S(2)}) collective-permute-start(f32[2,20,6,128]{3,2,1,0:T(8,128)S(1)} %get-tuple-element.32), channel_id=1, source_target_pairs={{0,2},{2,4},{4,6},{1,3},{3,5},{5,7},{8,10},{10,12},{12,14},{9,11},... | collective-permute-start | bytes 368648 | tf_op jit(solution)/shard_map/ppermute | solution.py:26
  30.7 7.2 %collective-permute-start.3 = (f32[2,20,6,128]{3,2,1,0:T(8,128)S(1)}, f32[2,20,6,128]{3,2,1,0:T(8,128)S(1)}, u32[]{:S(2)}, u32[]{:S(2)}) collective-permute-start(f32[2,20,6,128]{3,2,1,0:T(8,128)S(1)} %get-tuple-element.33), channel_id=1, source_target_pairs={{2,0},{4,2},{6,4},{3,1},{5,3},{7,5},{10,8},{12,10},{14,12},{11,9},... | collective-permute-start | bytes 368648 | tf_op jit(solution)/shard_map/ppermute | solution.py:29
  34.1 10.7 %collective-permute-start.10 = (f32[20,28,6]{2,1,0:T(8,128)}, f32[20,28,6]{2,1,0:T(8,128)}, u32[]{:S(2)}, u32[]{:S(2)}) collective-permute-start(f32[20,28,6]{2,1,0:T(8,128)} %get-tuple-element.30), channel_id=1, source_target_pairs={{0,1},{2,3},{4,5},{6,7},{8,9},{10,11},{12,13},{14,15},{16,17},{18,... | collective-permute-start | bytes 40328 | tf_op jit(solution)/shard_map/ppermute | solution.py:26
  36.1 8.7 %collective-permute-start.11 = (f32[20,28,6]{2,1,0:T(8,128)S(1)}, f32[20,28,6]{2,1,0:T(8,128)}, u32[]{:S(2)}, u32[]{:S(2)}) collective-permute-start(f32[20,28,6]{2,1,0:T(8,128)S(1)} %get-tuple-element.31), channel_id=1, source_target_pairs={{1,0},{3,2},{5,4},{7,6},{9,8},{11,10},{13,12},{15,14},{17,16},{19,... | collective-permute-start | bytes 40328 | tf_op jit(solution)/shard_map/ppermute | solution.py:29
  39.6 8.0 %collective-permute-start.5 = (f32[2,20,28,6]{2,0,3,1:T(2,128)S(1)}, f32[2,20,28,6]{2,0,3,1:T(2,128)S(1)}, u32[]{:S(2)}, u32[]{:S(2)}) collective-permute-start(f32[2,20,28,6]{2,0,3,1:T(2,128)S(1)} %copy.30), channel_id=1, source_target_pairs={{1,0},{3,2},{5,4},{7,6},{9,8},{11,10},{13,12},{15,14},{17,16},{19,... | collective-permute-start | bytes 80648 | tf_op jit(solution)/shard_map/ppermute | solution.py:29
  40.9 5.4 collective-permute-start.4
  70.8 43.0 %copy-start.3 = (f32[13,13]{1,0:T(8,128)S(1)}, f32[13,13]{1,0:T(8,128)}, u32[]{:S(2)}) copy-start(f32[13,13]{1,0:T(8,128)} %constant.156.clone) | copy-start | bytes 2032
  118.2 18.6 %copy-start.36 = (f32[13]{0:T(128)}, f32[13]{0:T(128)S(1)}, u32[]{:S(2)}) copy-start(f32[13]{0:T(128)S(1)} %multiply_add_fusion.19) | copy-start | bytes 160
  136.8 8.6 %collective-permute-start.12 = (f32[2,6,16,128]{3,2,1,0:T(8,128)S(1)}, f32[2,6,16,128]{3,2,1,0:T(8,128)S(1)}, u32[]{:S(2)}, u32[]{:S(2)}) collective-permute-start(f32[2,6,16,128]{3,2,1,0:T(8,128)S(1)} %get-tuple-element.42), channel_id=1, source_target_pairs={{0,8},{8,16},{16,24},{24,32},{32,40},{40,48},{48,56},{56,64},{64,7... | collective-permute-start | bytes 294920 | tf_op jit(solution)/shard_map/ppermute | solution.py:26
  138.7 8.2 %collective-permute-start.13 = (f32[2,6,16,128]{3,2,1,0:T(8,128)S(1)}, f32[2,6,16,128]{3,2,1,0:T(8,128)S(1)}, u32[]{:S(2)}, u32[]{:S(2)}) collective-permute-start(f32[2,6,16,128]{3,2,1,0:T(8,128)S(1)} %get-tuple-element.43), channel_id=1, source_target_pairs={{8,0},{16,8},{24,16},{32,24},{40,32},{48,40},{56,48},{64,56},{72,6... | collective-permute-start | bytes 294920 | tf_op jit(solution)/shard_map/ppermute | solution.py:29
  147.0 7.4 %collective-permute-start.14 = (f32[2,20,6,128]{3,2,1,0:T(8,128)S(1)}, f32[2,20,6,128]{3,2,1,0:T(8,128)S(1)}, u32[]{:S(2)}, u32[]{:S(2)}) collective-permute-start(f32[2,20,6,128]{3,2,1,0:T(8,128)S(1)} %get-tuple-element.28), channel_id=1, source_target_pairs={{0,2},{2,4},{4,6},{1,3},{3,5},{5,7},{8,10},{10,12},{12,14},{9,11},... | collective-permute-start | bytes 368648 | tf_op jit(solution)/shard_map/ppermute | solution.py:26
  150.3 7.2 %collective-permute-start.15 = (f32[2,20,6,128]{3,2,1,0:T(8,128)S(1)}, f32[2,20,6,128]{3,2,1,0:T(8,128)S(1)}, u32[]{:S(2)}, u32[]{:S(2)}) collective-permute-start(f32[2,20,6,128]{3,2,1,0:T(8,128)S(1)} %get-tuple-element.29), channel_id=1, source_target_pairs={{2,0},{4,2},{6,4},{3,1},{5,3},{7,5},{10,8},{12,10},{14,12},{11,9},... | collective-permute-start | bytes 368648 | tf_op jit(solution)/shard_map/ppermute | solution.py:29
  161.4 4.2 collective-permute-start.16
  164.3 3.6 collective-permute-start.17
  242.2 19.6 %copy-start.43 = (f32[13]{0:T(128)}, f32[13]{0:T(128)S(1)}, u32[]{:S(2)}) copy-start(f32[13]{0:T(128)S(1)} %multiply_add_fusion.15) | copy-start | bytes 160
  255.1 16.8 %copy-start.28 = (f32[13]{0:T(128)}, f32[13]{0:T(128)S(1)}, u32[]{:S(2)}) copy-start(f32[13]{0:T(128)S(1)} %multiply_add_fusion.12) | copy-start | bytes 160
  261.8 8.6 %collective-permute-start.18 = (f32[2,6,16,128]{3,2,1,0:T(8,128)S(1)}, f32[2,6,16,128]{3,2,1,0:T(8,128)S(1)}, u32[]{:S(2)}, u32[]{:S(2)}) collective-permute-start(f32[2,6,16,128]{3,2,1,0:T(8,128)S(1)} %get-tuple-element.40), channel_id=1, source_target_pairs={{0,8},{8,16},{16,24},{24,32},{32,40},{40,48},{48,56},{56,64},{64,7... | collective-permute-start | bytes 294920 | tf_op jit(solution)/shard_map/ppermute | solution.py:26
  263.7 8.2 %collective-permute-start.19 = (f32[2,6,16,128]{3,2,1,0:T(8,128)S(1)}, f32[2,6,16,128]{3,2,1,0:T(8,128)S(1)}, u32[]{:S(2)}, u32[]{:S(2)}) collective-permute-start(f32[2,6,16,128]{3,2,1,0:T(8,128)S(1)} %get-tuple-element.41), channel_id=1, source_target_pairs={{8,0},{16,8},{24,16},{32,24},{40,32},{48,40},{56,48},{64,56},{72,6... | collective-permute-start | bytes 294920 | tf_op jit(solution)/shard_map/ppermute | solution.py:29
  272.0 7.2 %collective-permute-start.20 = (f32[2,20,6,128]{3,2,1,0:T(8,128)S(1)}, f32[2,20,6,128]{3,2,1,0:T(8,128)S(1)}, u32[]{:S(2)}, u32[]{:S(2)}) collective-permute-start(f32[2,20,6,128]{3,2,1,0:T(8,128)S(1)} %get-tuple-element.26), channel_id=1, source_target_pairs={{0,2},{2,4},{4,6},{1,3},{3,5},{5,7},{8,10},{10,12},{12,14},{9,11},... | collective-permute-start | bytes 368648 | tf_op jit(solution)/shard_map/ppermute | solution.py:26
  273.9 7.2 %collective-permute-start.21 = (f32[2,20,6,128]{3,2,1,0:T(8,128)S(1)}, f32[2,20,6,128]{3,2,1,0:T(8,128)S(1)}, u32[]{:S(2)}, u32[]{:S(2)}) collective-permute-start(f32[2,20,6,128]{3,2,1,0:T(8,128)S(1)} %get-tuple-element.27), channel_id=1, source_target_pairs={{2,0},{4,2},{6,4},{3,1},{5,3},{7,5},{10,8},{12,10},{14,12},{11,9},... | collective-permute-start | bytes 368648 | tf_op jit(solution)/shard_map/ppermute | solution.py:29
  285.2 5.5 collective-permute-start.22
  289.2 3.6 collective-permute-start.23
  365.1 19.5 %copy-start.49 = (f32[13]{0:T(128)}, f32[13]{0:T(128)S(1)}, u32[]{:S(2)}) copy-start(f32[13]{0:T(128)S(1)} %bitcast_add_fusion.4) | copy-start | bytes 160
  387.7 23.0 %copy-start.4 = (f32[1,8,16,128]{3,0,2,1:T(1,128)}, f32[1,8,16,128]{3,0,2,1:T(1,128)S(1)}, u32[]{:S(2)}) copy-start(f32[1,8,16,128]{3,0,2,1:T(1,128)S(1)} %fusion.8) | copy-start | bytes 196612
  391.3 19.4 %copy-start.5 = (f32[1,8,16,128]{3,0,2,1:T(1,128)}, f32[1,8,16,128]{3,0,2,1:T(1,128)S(1)}, u32[]{:S(2)}) copy-start(f32[1,8,16,128]{3,0,2,1:T(1,128)S(1)} %fusion.10) | copy-start | bytes 196612
  391.3 8.6 %collective-permute-start.24 = (f32[2,6,16,128]{3,2,1,0:T(8,128)S(1)}, f32[2,6,16,128]{3,2,1,0:T(8,128)S(1)}, u32[]{:S(2)}, u32[]{:S(2)}) collective-permute-start(f32[2,6,16,128]{3,2,1,0:T(8,128)S(1)} %get-tuple-element.38), channel_id=1, source_target_pairs={{0,8},{8,16},{16,24},{24,32},{32,40},{40,48},{48,56},{56,64},{64,7... | collective-permute-start | bytes 294920 | tf_op jit(solution)/shard_map/ppermute | solution.py:26
  393.3 8.2 %collective-permute-start.25 = (f32[2,6,16,128]{3,2,1,0:T(8,128)S(1)}, f32[2,6,16,128]{3,2,1,0:T(8,128)S(1)}, u32[]{:S(2)}, u32[]{:S(2)}) collective-permute-start(f32[2,6,16,128]{3,2,1,0:T(8,128)S(1)} %get-tuple-element.39), channel_id=1, source_target_pairs={{8,0},{16,8},{24,16},{32,24},{40,32},{48,40},{56,48},{64,56},{72,6... | collective-permute-start | bytes 294920 | tf_op jit(solution)/shard_map/ppermute | solution.py:29
  401.6 7.2 %collective-permute-start.26 = (f32[2,20,6,128]{3,2,1,0:T(8,128)S(1)}, f32[2,20,6,128]{3,2,1,0:T(8,128)S(1)}, u32[]{:S(2)}, u32[]{:S(2)}) collective-permute-start(f32[2,20,6,128]{3,2,1,0:T(8,128)S(1)} %get-tuple-element.24), channel_id=1, source_target_pairs={{0,2},{2,4},{4,6},{1,3},{3,5},{5,7},{8,10},{10,12},{12,14},{9,11},... | collective-permute-start | bytes 368648 | tf_op jit(solution)/shard_map/ppermute | solution.py:26
  403.5 7.2 %collective-permute-start.27 = (f32[2,20,6,128]{3,2,1,0:T(8,128)S(1)}, f32[2,20,6,128]{3,2,1,0:T(8,128)S(1)}, u32[]{:S(2)}, u32[]{:S(2)}) collective-permute-start(f32[2,20,6,128]{3,2,1,0:T(8,128)S(1)} %get-tuple-element.25), channel_id=1, source_target_pairs={{2,0},{4,2},{6,4},{3,1},{5,3},{7,5},{10,8},{12,10},{14,12},{11,9},... | collective-permute-start | bytes 368648 | tf_op jit(solution)/shard_map/ppermute | solution.py:29
  415.6 9.0 %collective-permute-start.29 = (f32[2,20,28,6]{2,0,3,1:T(2,128)S(1)}, f32[2,20,28,6]{2,0,3,1:T(2,128)}, u32[]{:S(2)}, u32[]{:S(2)}) collective-permute-start(f32[2,20,28,6]{2,0,3,1:T(2,128)S(1)} %copy.58), channel_id=1, source_target_pairs={{1,0},{3,2},{5,4},{7,6},{9,8},{11,10},{13,12},{15,14},{17,16},{19,... | collective-permute-start | bytes 80648 | tf_op jit(solution)/shard_map/ppermute | solution.py:29
  416.9 6.4 collective-permute-start.28
  448.2 41.8 %copy-start.21 = (f32[1,13]{1,0:T(1,128)S(1)}, f32[1,13]{1,0:T(1,128)}, u32[]{:S(2)}) copy-start(f32[1,13]{1,0:T(1,128)} %copy-done.20) | copy-start | bytes 160
  448.2 41.8 %copy-start.24 = (pred[13,13]{1,0:T(8,128)(4,1)S(1)}, pred[13,13]{1,0:T(8,128)(4,1)}, u32[]{:S(2)}) copy-start(pred[13,13]{1,0:T(8,128)(4,1)} %copy-done.23) | copy-start | bytes 511
  494.9 19.6 %copy-start.57 = (f32[13]{0:T(128)}, f32[13]{0:T(128)S(1)}, u32[]{:S(2)}) copy-start(f32[13]{0:T(128)S(1)} %bitcast_add_fusion.2) | copy-start | bytes 160
  508.8 18.2 %copy-start.29 = (f32[13]{0:T(128)S(1)}, f32[13]{0:T(128)}, u32[]{:S(2)}) copy-start(f32[13]{0:T(128)} %copy-done.28) | copy-start | bytes 160
  508.8 18.3 %copy-start.42 = (f32[13]{0:T(128)S(1)}, f32[13]{0:T(128)}, u32[]{:S(2)}) copy-start(f32[13]{0:T(128)} %copy-done.41) | copy-start | bytes 160
  508.8 18.3 %copy-start.44 = (f32[13]{0:T(128)S(1)}, f32[13]{0:T(128)}, u32[]{:S(2)}) copy-start(f32[13]{0:T(128)} %copy-done.43) | copy-start | bytes 160
  508.8 18.3 %copy-start.46 = (f32[13]{0:T(128)S(1)}, f32[13]{0:T(128)}, u32[]{:S(2)}) copy-start(f32[13]{0:T(128)} %copy-done.45) | copy-start | bytes 160
  508.8 18.3 %copy-start.48 = (f32[13]{0:T(128)S(1)}, f32[13]{0:T(128)}, u32[]{:S(2)}) copy-start(f32[13]{0:T(128)} %copy-done.47) | copy-start | bytes 160
  518.8 16.3 %copy-start.1 = (f32[13,8,16,128]{3,2,1,0:T(8,128)S(1)}, f32[13,8,16,128]{3,2,1,0:T(8,128)}, u32[]{:S(2)}) copy-start(f32[13,8,16,128]{3,2,1,0:T(8,128)} %copy-done) | copy-start | bytes 2555908
  518.9 16.3 %copy-start.31 = (f32[13]{0:T(128)S(1)}, f32[13]{0:T(128)}, u32[]{:S(2)}) copy-start(f32[13]{0:T(128)} %copy-done.30) | copy-start | bytes 160
  518.9 16.3 %copy-start.50 = (f32[13]{0:T(128)S(1)}, f32[13]{0:T(128)}, u32[]{:S(2)}) copy-start(f32[13]{0:T(128)} %copy-done.49) | copy-start | bytes 160
  518.9 16.3 %copy-start.52 = (f32[13]{0:T(128)S(1)}, f32[13]{0:T(128)}, u32[]{:S(2)}) copy-start(f32[13]{0:T(128)} %copy-done.51) | copy-start | bytes 160
  518.9 16.3 %copy-start.54 = (f32[13]{0:T(128)S(1)}, f32[13]{0:T(128)}, u32[]{:S(2)}) copy-start(f32[13]{0:T(128)} %copy-done.53) | copy-start | bytes 160
  518.9 9.3 %collective-permute-start.30 = (f32[2,6,16,128]{3,2,1,0:T(8,128)S(1)}, f32[2,6,16,128]{3,2,1,0:T(8,128)S(1)}, u32[]{:S(2)}, u32[]{:S(2)}) collective-permute-start(f32[2,6,16,128]{3,2,1,0:T(8,128)S(1)} %get-tuple-element.36), channel_id=1, source_target_pairs={{0,8},{8,16},{16,24},{24,32},{32,40},{40,48},{48,56},{56,64},{64,7... | collective-permute-start | bytes 294920 | tf_op jit(solution)/shard_map/ppermute | solution.py:26
  521.0 8.2 %collective-permute-start.31 = (f32[2,6,16,128]{3,2,1,0:T(8,128)S(1)}, f32[2,6,16,128]{3,2,1,0:T(8,128)S(1)}, u32[]{:S(2)}, u32[]{:S(2)}) collective-permute-start(f32[2,6,16,128]{3,2,1,0:T(8,128)S(1)} %get-tuple-element.37), channel_id=1, source_target_pairs={{8,0},{16,8},{24,16},{32,24},{40,32},{48,40},{56,48},{64,56},{72,6... | collective-permute-start | bytes 294920 | tf_op jit(solution)/shard_map/ppermute | solution.py:29
  529.3 7.2 %collective-permute-start.32 = (f32[2,20,6,128]{3,2,1,0:T(8,128)S(1)}, f32[2,20,6,128]{3,2,1,0:T(8,128)S(1)}, u32[]{:S(2)}, u32[]{:S(2)}) collective-permute-start(f32[2,20,6,128]{3,2,1,0:T(8,128)S(1)} %get-tuple-element.22), channel_id=1, source_target_pairs={{0,2},{2,4},{4,6},{1,3},{3,5},{5,7},{8,10},{10,12},{12,14},{9,11},... | collective-permute-start | bytes 368648 | tf_op jit(solution)/shard_map/ppermute | solution.py:26
  531.2 7.2 %collective-permute-start.33 = (f32[2,20,6,128]{3,2,1,0:T(8,128)S(1)}, f32[2,20,6,128]{3,2,1,0:T(8,128)S(1)}, u32[]{:S(2)}, u32[]{:S(2)}) collective-permute-start(f32[2,20,6,128]{3,2,1,0:T(8,128)S(1)} %get-tuple-element.23), channel_id=1, source_target_pairs={{2,0},{4,2},{6,4},{3,1},{5,3},{7,5},{10,8},{12,10},{14,12},{11,9},... | collective-permute-start | bytes 368648 | tf_op jit(solution)/shard_map/ppermute | solution.py:29
  542.7 8.8 %collective-permute-start.35 = (f32[2,20,28,6]{2,0,3,1:T(2,128)S(1)}, f32[2,20,28,6]{2,0,3,1:T(2,128)}, u32[]{:S(2)}, u32[]{:S(2)}) collective-permute-start(f32[2,20,28,6]{2,0,3,1:T(2,128)S(1)} %copy.64), channel_id=1, source_target_pairs={{1,0},{3,2},{5,4},{7,6},{9,8},{11,10},{13,12},{15,14},{17,16},{19,... | collective-permute-start | bytes 80648 | tf_op jit(solution)/shard_map/ppermute | solution.py:29
  544.0 6.3 collective-permute-start.34
  574.7 42.2 %copy-start.22 = (f32[1,13]{1,0:T(1,128)S(1)}, f32[1,13]{1,0:T(1,128)}, u32[]{:S(2)}) copy-start(f32[1,13]{1,0:T(1,128)} %copy-done.20) | copy-start | bytes 160
  574.7 42.2 %copy-start.25 = (pred[13,13]{1,0:T(8,128)(4,1)S(1)}, pred[13,13]{1,0:T(8,128)(4,1)}, u32[]{:S(2)}) copy-start(pred[13,13]{1,0:T(8,128)(4,1)} %copy-done.23) | copy-start | bytes 511
  576.9 68.3 %copy-start.18 = (f32[1,8,16,128]{3,0,2,1:T(1,128)S(1)}, f32[1,8,16,128]{3,0,2,1:T(1,128)}, u32[]{:S(2)}) copy-start(f32[1,8,16,128]{3,0,2,1:T(1,128)} %fusion.438) | copy-start | bytes 196612
  576.9 68.3 %copy-start.19 = (f32[1,8,16,128]{3,0,2,1:T(1,128)S(1)}, f32[1,8,16,128]{3,0,2,1:T(1,128)}, u32[]{:S(2)}) copy-start(f32[1,8,16,128]{3,0,2,1:T(1,128)} %fusion.4) | copy-start | bytes 196612
  (37 other events, 317.9 us)
where the time goes:
time: 659 us; the launch traced here: 646 us
  blocking collectives  194 us (29%)
  starting transfers between devices  111 us (17%)
  other arithmetic  111 us (17%)
  between operations  82.9 us (13%)
  matrix products  79.3 us (12%)
  local copies, waits for them, and re-layouts  45.6 us (7%)
  waiting for transfers between devices  22.2 us (3%)
    psum x20, blocking collectives, over_axes(): return functools.reduce(lax.psum, axes, shard)  194 us
    ppermute x18, starting transfers between devices, extended_2(): lax.ppermute(lax.slice_in_dim(block, 0, width, axis=dim), axis, backward)  65.1 us
    sub x37, other arithmetic, chebyshev_next(): return 2.0 * scaled - previous  63.6 us
    ppermute x18, starting transfers between devices, extended_2(): lax.ppermute(lax.slice_in_dim(block, block.shape[dim] - width, None, axis...  46.2 us
    div x10, other arithmetic, chebyshev_next(): scaled = (images - center_shift * current) / half_width  31 us
    dot_general x30, matrix products, coefficients(): jnp.dot(gram_matrix, moved, precision=lax.Precision.HIGHEST)  22.7 us
    dot_general x30, matrix products, coefficients(): jnp.dot(gram_matrix, res_coeff, precision=lax.Precision.HIGHEST)  22.3 us
    dot_general x14, matrix products, combine(): jnp.tensordot(coeff, basis_set, axes=1, precision=lax.Precision.HIGHEST)  19 us
  transfers between devices with their start and end apart: 36, of which 17 were waited for; matrix products, arithmetic and copies ran while one was open for 3% of the time, Pallas kernels for 0%

commit v1 on v0

v1 whole, which is shorter than its diff:
```python
import functools

import jax
import jax.numpy as jnp
import numpy as np
from jax import lax
from jax.experimental import pallas as pl
from jax.experimental.pallas import tpu as pltpu
from jax.sharding import PartitionSpec as P

S = 6
OUTER = 5
MESH = pl.DeviceIdType.MESH

CENTER = 19.0
HALF = 19.0

BZ = 8
NZE = BZ + 2 * S
ROWS = 40
LO, MID, HI = 8, 16, 24

NPP, NPR, NRR = 2 * S + 1, 2 * S, 2 * S - 1


def weights():
    columns = 2 * S + 1
    total = NPP + NPR + NRR

    def moment(offset, m):
        v = np.zeros(total)
        if m < 2:
            v[offset + m] = 1.0
        else:
            v[offset + m] = 2.0
            v[offset + m % 2] -= 1.0
        return v

    gram = np.zeros((columns, columns, total))
    for i in range(columns):
        for j in range(columns):
            di, dj = (i if i <= S else i - S - 1), (j if j <= S else j - S - 1)
            kinds = (i > S) + (j > S)
            offset = (0, NPP, NPP + NPR)[kinds]
            gram[i, j] = (moment(offset, di + dj) + moment(offset, abs(di - dj))) / 2
    change = np.zeros((columns, columns))
    for offset, length in ((0, S), (S + 1, S - 1)):
        for degree in range(length):
            change[offset + degree, offset + degree] = CENTER
            if degree == 0:
                change[offset + 1, offset] = HALF
            else:
                change[offset + degree + 1, offset + degree] = 0.5 * HALF
                change[offset + degree - 1, offset + degree] = 0.5 * HALF
    moved = np.einsum("ikm,kj->ijm", gram, change)
    out = np.zeros((2, columns, 2, 8, 128), np.float32)
    for which, table in enumerate((gram, moved)):
        for j in range(columns):
            for i in range(columns):
                half, row = (0, i) if i <= S else (1, i - S - 1)
                out[which, j, half, row, :total] = table[i, j]
    return out


def kernel(
    rhs_ref, diag_ref, w_ref, sol_ref, res_ref,
    F, PV, RV, C, M, V0, X, land, S1, S2,
    zs_sem, zr_sem, ys_sem, yr_sem, fs_sem, fr_sem, io_s, io_r, g1_s, g1_r, g2_s, g2_r,
):
    gz = lax.axis_index("gz")
    gy = lax.axis_index("gy")
    gx = lax.axis_index("gx")
    nz = lax.axis_size("gz")
    ny = lax.axis_size("gy")
    yv = 2 * gy + gx
    nyv = 2 * ny
    sib = 1 - gx
    nzp = 8
    py = gz // nzp
    pz = gz % nzp

    own_rows = pl.ds(MID, 8)
    own_z = pl.ds(S, BZ)

    swaps = []
    for f, ref in enumerate((rhs_ref, diag_ref)):
        cp = pltpu.make_async_remote_copy(
            src_ref=ref.at[:, pl.ds(pl.multiple_of(8 * sib, 8), 8), :],
            dst_ref=F.at[f, gx, own_z, own_rows, :],
            send_sem=io_s.at[f], recv_sem=io_r.at[f],
            device_id=(gz, gy, sib), device_id_type=MESH,
        )
        cp.start()
        swaps.append(cp)
        F[f, gx, S:S + BZ, MID:MID + 8, :] = ref[:, pl.ds(pl.multiple_of(8 * gx, 8), 8), :]

    @pl.when(gz == 0)
    def _():
        F[:, :, 0:S, :, :] = jnp.zeros((2, 2, S, ROWS, 128), jnp.float32)

    @pl.when(gz == nz - 1)
    def _():
        F[:, :, S + BZ:NZE, :, :] = jnp.zeros((2, 2, S, ROWS, 128), jnp.float32)

    @pl.when(yv == 0)
    def _():
        F[:, :, :, LO:MID, :] = jnp.zeros((2, 2, NZE, 8, 128), jnp.float32)

    @pl.when(yv == nyv - 1)
    def _():
        F[:, :, :, HI:HI + 8, :] = jnp.zeros((2, 2, NZE, 8, 128), jnp.float32)

    X[...] = jnp.zeros(X.shape, jnp.float32)

    row = lax.broadcasted_iota(jnp.int32, (24, 128), 0) + (8 * yv - 8)
    row_in = jnp.where((row >= 0) & (row < 8 * nyv), 2.0 / HALF, 0.0)
    for z in range(NZE):
        at = gz * BZ + (z - S)
        M[z] = row_in * jnp.where((at >= 0) & (at < nz * BZ), 1.0, 0.0)

    for cp in swaps:
        cp.wait()

    lane = lax.broadcasted_iota(jnp.int32, (24, 128), 1)

    def x_sum(v, rows):
        first = lane[:rows] == 0
        last = lane[:rows] == 127
        a0, a1 = pltpu.roll(v[0], 1, 1), pltpu.roll(v[1], 1, 1)
        b0, b1 = pltpu.roll(v[0], 127, 1), pltpu.roll(v[1], 127, 1)
        zero = jnp.zeros((rows, 128), jnp.float32)
        s0 = v[0] + jnp.where(first, zero, a0) + jnp.where(last, b1, b0)
        s1 = v[1] + jnp.where(first, a0, a1) + jnp.where(last, zero, b1)
        return s0, s1

    def neighbours(dz=0, dy=0):
        t = yv + dy
        return (gz + dz, t // 2, t % 2)

    def z_copy(k):
        src, dst, dz = ((S, S + BZ, -1), (BZ, 0, 1))[k]
        return pltpu.make_async_remote_copy(
            src_ref=F.at[:, :, pl.ds(src, S), own_rows, :],
            dst_ref=F.at[:, :, pl.ds(dst, S), own_rows, :],
            send_sem=zs_sem.at[k], recv_sem=zr_sem.at[k],
            device_id=neighbours(dz=dz), device_id_type=MESH,
        )

    def y_copy(k, planes, send, recv):
        dst, dy = ((HI, -1), (LO, 1))[k]
        return pltpu.make_async_remote_copy(
            src_ref=F.at[:, :, planes, own_rows, :],
            dst_ref=F.at[:, :, planes, pl.ds(dst, 8), :],
            send_sem=send, recv_sem=recv,
            device_id=neighbours(dy=dy), device_id_type=MESH,
        )

    to_z = (gz > 0, gz < nz - 1)
    from_z = (gz < nz - 1, gz > 0)
    to_y = (yv > 0, yv < nyv - 1)
    from_y = (yv < nyv - 1, yv > 0)
    bands = (pl.ds(S + BZ, S), pl.ds(0, S))

    def exchange():
        for k in range(2):
            @pl.when(to_z[k])
            def _(k=k):
                z_copy(k).start()
        for k in range(2):
            @pl.when(to_y[k])
            def _(k=k):
                y_copy(k, own_z, ys_sem.at[k], yr_sem.at[k]).start()
        for b in range(2):
            @pl.when(from_z[b])
            def _(b=b):
                z_copy(b).wait_recv()
                for k in range(2):
                    @pl.when(to_y[k])
                    def _(k=k):
                        y_copy(k, bands[b], fs_sem.at[b, k], fr_sem.at[b, k]).start()
        for k in range(2):
            @pl.when(from_y[k])
            def _(k=k):
                y_copy(k, own_z, ys_sem.at[k], yr_sem.at[k]).wait_recv()
                for b in range(2):
                    @pl.when(from_z[b])
                    def _(b=b):
                        y_copy(k, bands[b], fs_sem.at[b, k], fr_sem.at[b, k]).wait_recv()
        for k in range(2):
            @pl.when(to_z[k])
            def _(k=k):
                z_copy(k).wait_send()

            @pl.when(to_y[k])
            def _(k=k):
                y_copy(k, own_z, ys_sem.at[k], yr_sem.at[k]).wait_send()
                for b in range(2):
                    @pl.when(from_z[b])
                    def _(b=b):
                        y_copy(k, bands[b], fs_sem.at[b, k], fr_sem.at[b, k]).wait_send()

    def power_steps(read, write, degree, z0, z1, rows):
        r0, n = rows
        m0 = r0 - LO
        sums = {}

        def y_sum(z):
            if z not in sums:
                sums[z] = (
                    read(degree - 1, z, r0 - 1, n) + read(degree - 1, z, r0, n) + read(degree - 1, z, r0 + 1, n)
                )
            return sums[z]

        for z in range(z0, z1):
            s0, s1 = x_sum(y_sum(z - 1) + y_sum(z) + y_sum(z + 1), n)
            sums.pop(z - 1, None)
            mask = M[z, m0:m0 + n, :]
            box = jnp.stack([s0 * mask, s1 * mask])
            value = C[:, z, r0:r0 + n, :] * read(degree - 1, z, r0, n) - box
            if degree == 1:
                value = 0.5 * value
            else:
                value = value - read(degree - 2, z, r0, n)
            write(degree, z, r0, n, value)

    def reader(f, V):
        def read(degree, z, r, n):
            if degree == 0:
                return F[f, :, z, r:r + n, :]
            return V[degree - 1, :, z, r:r + n, :]
        return read

    def writer(V):
        def write(degree, z, r, n, value):
            V[degree - 1, :, z, r:r + n, :] = value
        return write

    read_p, read_r = reader(0, PV), reader(1, RV)
    write_p, write_r = writer(PV), writer(RV)

    def own(block, degree, xt):
        if degree == 0:
            return V0[block, xt]
        V = (PV, RV)[block]
        return V[degree - 1, xt, S:S + BZ, MID:MID + 8, :]

    lane8 = lax.broadcasted_iota(jnp.int32, (8, 128), 1)
    sub8 = lax.broadcasted_iota(jnp.int32, (8, 128), 0)

    def all_sublanes(v):
        v = v + pltpu.roll(v, 4, 0)
        v = v + pltpu.roll(v, 2, 0)
        return v + pltpu.roll(v, 1, 0)

    def splat(v, j):
        return jnp.broadcast_to(v[j:j + 1, :], (8, 128))

    def by_row(values):
        out = jnp.zeros((8, 128), jnp.float32)
        for j, value in enumerate(values):
            if value:
                out = jnp.where(sub8 == j, value, out)
        return out

    diag_c = (by_row([CENTER] * S), by_row([CENTER] * (S - 1)))
    from_low = (by_row([0.0, HALF] + [0.5 * HALF] * (S - 1)), by_row([0.0, HALF] + [0.5 * HALF] * (S - 2)))
    from_high = (by_row([0.5 * HALF] * (S - 1)), by_row([0.5 * HALF] * (S - 2)))

    def outer(t, carry):
        par = t % 2
        exchange()

        @pl.when(t == 0)
        def _():
            for z in range(NZE):
                C[:, z, LO:HI + 8, :] = (2.0 / HALF) * (
                    F[1, :, z, LO:HI + 8, :] + (27.0 - CENTER)
                )
                F[1, :, z, LO:HI + 8, :] = F[0, :, z, LO:HI + 8, :]

        for f in range(2):
            V0[f] = F[f, :, S:S + BZ, MID:MID + 8, :]
        for degree in range(1, S + 1):
            rows = (LO, 24) if degree < S else (MID, 8)
            power_steps(read_p, write_p, degree, degree, NZE - degree, rows)
            if degree < S:
                rows = (LO, 24) if degree < S - 1 else (MID, 8)
                power_steps(read_r, write_r, degree, degree + 1, NZE - degree - 1, rows)

        parts = [None] * (NPP + NPR + NRR)

        def add(k, a, b):
            s = jnp.sum(a * b, axis=0)
            parts[k] = s if parts[k] is None else parts[k] + s

        for xt in range(2):
            p, r = own(0, 0, xt), own(1, 0, xt)
            for i in range(S + 1):
                p_next = own(0, i + 1, xt) if i < S else None
                r_next = own(1, i + 1, xt) if i < S - 1 else None
                add(2 * i, p, p)
                if i < S:
                    add(2 * i + 1, p, p_next)
                    add(NPP + 2 * i, p, r)
                    add(NPP + 2 * i + 1, p_next, r)
                    add(NPP + NPR + 2 * i, r, r)
                if i < S - 1:
                    add(NPP + NPR + 2 * i + 1, r, r_next)
                p, r = p_next, r_next
        picked = jnp.zeros((8, 128), jnp.float32)
        for k, part in enumerate(parts):
            picked = jnp.where(lane8 == k, jnp.sum(part, axis=1, keepdims=True), picked)
        local = jnp.sum(picked, axis=0, keepdims=True)

        me1 = 8 * py + yv
        S1[par, me1] = local
        for dy in range(4):
            for dx in range(4):
                for dc in range(2):
                    if dy or dx or dc:
                        to = (((py + dy) % 4) * nzp + pz, (gy + dx) % 4, (gx + dc) % 2)
                        pltpu.make_async_remote_copy(
                            src_ref=S1.at[par, me1], dst_ref=S1.at[par, me1],
                            send_sem=g1_s.at[par], recv_sem=g1_r.at[par],
                            device_id=to, device_id_type=MESH,
                        ).start()
        whole1 = pltpu.make_async_copy(S1.at[par, pl.ds(0, 31)], S1.at[par, pl.ds(0, 31)], g1_r.at[par])
        whole1.wait()
        S2[par, pz] = jnp.sum(S1[par], axis=0)
        for dz in range(1, nzp):
            to = (py * nzp + (pz + dz) % nzp, gy, gx)
            pltpu.make_async_remote_copy(
                src_ref=S2.at[par, pz], dst_ref=S2.at[par, pz],
                send_sem=g2_s.at[par], recv_sem=g2_r.at[par],
                device_id=to, device_id_type=MESH,
            ).start()
        whole2 = pltpu.make_async_copy(S2.at[par, pl.ds(0, 7)], S2.at[par, pl.ds(0, 7)], g2_r.at[par])
        whole2.wait()
        moments = jnp.broadcast_to(jnp.sum(S2[par], axis=0), (8, 128))
        pltpu.make_async_copy(S1.at[par, pl.ds(0, 31)], S1.at[par, pl.ds(0, 31)], g1_s.at[par]).wait()
        pltpu.make_async_copy(S2.at[par, pl.ds(0, 7)], S2.at[par, pl.ds(0, 7)], g2_s.at[par]).wait()

        columns = 2 * S + 1
        table = [
            [
                [
                    jnp.broadcast_to(jnp.sum(w_ref[which, j, half] * moments, axis=1, keepdims=True), (8, 128))
                    for half in range(2)
                ]
                for j in range(columns)
            ]
            for which in range(2)
        ]

        def form(which, v):
            col = [splat(v[0], j) for j in range(S + 1)] + [splat(v[1], j) for j in range(S)]
            total = None
            for half in range(2):
                terms = [table[which][j][half] * col[j] for j in range(columns)]
                while len(terms) > 1:
                    terms = [
                        terms[i] + terms[i + 1] if i + 1 < len(terms) else terms[i] for i in range(0, len(terms), 2)
                    ]
                part = terms[0] * v[half]
                total = part if total is None else total + part
            return all_sublanes(total)

        unit = jnp.where(sub8 == 0, 1.0, 0.0)
        none = jnp.zeros((8, 128), jnp.float32)
        p_c, r_c, x_c = [unit, none], [none, unit], [none, none]
        norm = form(0, r_c)
        for step in range(S):
            q = [
                diag_c[h] * p_c[h] + from_low[h] * pltpu.roll(p_c[h], 1, 0) + from_high[h] * pltpu.roll(p_c[h], 7, 0)
                for h in range(2)
            ]
            length = norm / form(1, p_c)
            x_c = [x_c[h] + length * p_c[h] for h in range(2)]
            r_c = [r_c[h] - length * q[h] for h in range(2)]
            norm_next = form(0, r_c)
            ratio = norm_next / norm
            p_c = [r_c[h] + ratio * p_c[h] for h in range(2)]
            norm = norm_next

        def combine(c, xt):
            total = None
            for block in range(2):
                for degree in range(S + 1 - block):
                    term = splat(c[block], degree)[None] * own(block, degree, xt)
                    total = term if total is None else total + term
            return total

        for xt in range(2):
            F[0, xt, S:S + BZ, MID:MID + 8, :] = combine(p_c, xt)
            F[1, xt, S:S + BZ, MID:MID + 8, :] = combine(r_c, xt)
            X[xt] = X[xt] + combine(x_c, xt)
        return carry

    lax.fori_loop(0, OUTER, outer, 0)

    backs = []
    for f, (src, out) in enumerate(
        ((X.at[sib], sol_ref), (F.at[1, sib, own_z, own_rows, :], res_ref))
    ):
        cp = pltpu.make_async_remote_copy(
            src_ref=src, dst_ref=land.at[f],
            send_sem=io_s.at[2 + f], recv_sem=io_r.at[2 + f],
            device_id=(gz, gy, sib), device_id_type=MESH,
        )
        cp.start()
        backs.append(cp)
    mine = pl.ds(pl.multiple_of(8 * gx, 8), 8)
    sol_ref[:, mine, :] = X[gx]
    res_ref[:, mine, :] = F[1, gx, S:S + BZ, MID:MID + 8, :]
    other = pl.ds(pl.multiple_of(8 * sib, 8), 8)
    for f, out in enumerate((sol_ref, res_ref)):
        backs[f].wait()
        out[:, other, :] = land[f]


def solution(mesh):
    table = weights()

    def local(right_side, diagonal):
        f32 = jnp.float32
        dma = pltpu.SemaphoreType.DMA
        field = (2, NZE, ROWS, 128)
        return pl.pallas_call(
            kernel,
            out_shape=(jax.ShapeDtypeStruct(right_side.shape, f32),) * 2,
            in_specs=[pl.BlockSpec(memory_space=pltpu.VMEM)] * 3,
            out_specs=(pl.BlockSpec(memory_space=pltpu.VMEM),) * 2,
            scratch_shapes=[
                pltpu.VMEM((2,) + field, f32),
                pltpu.VMEM((S,) + field, f32),
                pltpu.VMEM((S - 1,) + field, f32),
                pltpu.VMEM(field, f32),
                pltpu.VMEM((NZE, 24, 128), f32),
                pltpu.VMEM((2, 2, BZ, 8, 128), f32),
                pltpu.VMEM((2, BZ, 8, 128), f32),
                pltpu.VMEM((2, BZ, 8, 128), f32),
                pltpu.VMEM((2, 32, 1, 128), f32),
                pltpu.VMEM((2, 8, 1, 128), f32),
                dma((2,)), dma((2,)), dma((2,)), dma((2,)), dma((2, 2)), dma((2, 2)),
                dma((4,)), dma((4,)), dma((2,)), dma((2,)), dma((2,)), dma((2,)),
            ],
            compiler_params=pltpu.CompilerParams(has_side_effects=True, vmem_limit_bytes=48 * 2**20),
        )(right_side, diagonal, jnp.asarray(table))

    spec = P("gz", "gy", "gx")
    return jax.shard_map(
        local, mesh=mesh, in_specs=(spec, spec), out_specs=(spec, spec), check_vma=False
    )
```

time: 659 us -> 125 us (0.19)
  the two profiles are of different devices: /device:TPU:10 before, /device:TPU:1 now
where the time goes in v1:
time: 125 us
  Pallas kernels  121 us (97%)
  local copies, waits for them, and re-layouts  3.87 us (3%)
    pallas_call x1, Pallas kernels, local(): pl.pallas_call(kernel, out_shape=(jax.ShapeDtypeStruct(right_side.shape,...  121 us
    unnamed x8, local copies, waits for them, and re-layouts  3.87 us

profile of v1, /device:TPU:1, one launch (start us, length us, event | category | flops | bytes accessed | tf_op | source)
XLA Modules:
  0.0 125.2 jit_solution(11201063140202419807)
XLA Ops:
  0.6 0.0 copy-start
  0.6 0.9 copy-done
  1.6 0.0 copy-start.1
  1.6 0.8 copy-done.1
  2.4 0.0 copy-start.2
  2.4 0.8 copy-done.2
  3.2 120.7 %shard_map.50 = (f32[8,16,128]{2,1,0:T(8,128)S(1)}, f32[8,16,128]{2,1,0:T(8,128)S(1)}) custom-call(f32[8,16,128]{2,1,0:T(8,128)S(1)} %copy-done.1, f32[8,16,128]{2,1,0:T(8,128)S(1)} %copy-done.2, f32[2,13,2,8,128]{4,3,2,1,0:T(8,128)S(1)} %copy-done), custom_call_target="tpu_custom_call" | custom-call | tf_op jit(solution)/shard_map/pallas_call | solution.py:428
  123.9 0.6 copy.7
  124.5 0.6 copy.8
Async XLA Ops:
  0.6 0.9 copy-start
  1.6 0.8 copy-start.1
  2.4 0.8 copy-start.2

commit v2 on v1

--- a/solution.py
+++ b/solution.py
@@ -9,7 +9,7 @@
 from jax.sharding import PartitionSpec as P
 
 S = 6
-OUTER = 5
+INNER = (6,) * 5
 MESH = pl.DeviceIdType.MESH
 
 CENTER = 19.0
@@ -21,6 +21,14 @@
 LO, MID, HI = 8, 16, 24
 
 NPP, NPR, NRR = 2 * S + 1, 2 * S, 2 * S - 1
+
+PARTS = 3 if S == 8 else 2
+
+
+def place(i):
+    if i > S:
+        return 1, i - S - 1
+    return (0, i) if i < 8 else (2, i - 8)
 
 
 def weights():
@@ -53,19 +61,19 @@
                 change[offset + degree + 1, offset + degree] = 0.5 * HALF
                 change[offset + degree - 1, offset + degree] = 0.5 * HALF
     moved = np.einsum("ikm,kj->ijm", gram, change)
-    out = np.zeros((2, columns, 2, 8, 128), np.float32)
+    out = np.zeros((2, columns, PARTS, 8, 128), np.float32)
     for which, table in enumerate((gram, moved)):
         for j in range(columns):
             for i in range(columns):
-                half, row = (0, i) if i <= S else (1, i - S - 1)
+                half, row = place(i)
                 out[which, j, half, row, :total] = table[i, j]
     return out
 
 
 def kernel(
-    rhs_ref, diag_ref, w_ref, sol_ref, res_ref,
-    F, PV, RV, C, M, V0, X, land, S1, S2,
-    zs_sem, zr_sem, ys_sem, yr_sem, fs_sem, fr_sem, io_s, io_r, g1_s, g1_r, g2_s, g2_r,
+    rhs_ref, diag_ref, w_hbm, sol_ref, res_ref,
+    F, PV, RV, C, M, V0, X, XC, land, S1, S2, w_ref,
+    in_sem, zs_sem, zr_sem, ys_sem, yr_sem, cs_sem, cr_sem, fs_sem, fr_sem, io_s, io_r, g1_s, g1_r, g2_s, g2_r,
 ):
     gz = lax.axis_index("gz")
     gy = lax.axis_index("gy")
@@ -81,44 +89,78 @@
 
     own_rows = pl.ds(MID, 8)
     own_z = pl.ds(S, BZ)
-
+    mine = pl.ds(pl.multiple_of(8 * gx, 8), 8)
+    other = pl.ds(pl.multiple_of(8 * sib, 8), 8)
+
+    loads = []
+    for f, ref in enumerate((rhs_ref, diag_ref)):
+        loads.append(pltpu.make_async_copy(ref.at[:, other, :], land.at[f], in_sem.at[f]))
+    for f, ref in enumerate((rhs_ref, diag_ref)):
+        loads.append(pltpu.make_async_copy(ref.at[:, mine, :], F.at[f, gx, own_z, own_rows, :], in_sem.at[2 + f]))
+    loads.append(pltpu.make_async_copy(w_hbm, w_ref, in_sem.at[4]))
+    for cp in loads:
+        cp.start()
+
+    plane = [
+        (((py + dy) % 4) * nzp + pz, (gy + dx) % 4, (gx + dc) % 2)
+        for dy in range(4) for dx in range(4) for dc in range(2) if dy or dx or dc
+    ]
+    line = [(py * nzp + (pz + dz) % nzp, gy, gx) for dz in range(1, nzp)]
+    off_gy = gy + 2 * gx - 1
+    has_off = (off_gy >= 0) & (off_gy < ny)
+    to_z = (gz > 0, gz < nz - 1)
+    from_z = (gz < nz - 1, gz > 0)
+
+    barrier = pltpu.get_barrier_semaphore()
+    for to in plane + line:
+        pl.semaphore_signal(barrier, inc=1, device_id=to, device_id_type=MESH)
+    for k, dz in enumerate((-1, 1)):
+        @pl.when(to_z[k])
+        def _(dz=dz):
+            pl.semaphore_signal(barrier, inc=1, device_id=(gz + dz, gy, gx), device_id_type=MESH)
+
+        @pl.when(to_z[k] & has_off)
+        def _(dz=dz):
+            pl.semaphore_signal(barrier, inc=1, device_id=(gz + dz, off_gy, sib), device_id_type=MESH)
+
+    @pl.when(gz == 0)
+    def _():
+        F[:, :, 0:S, :, :] = jnp.zeros((2, 2, S, ROWS, 128), jnp.float32)
+
+    @pl.when(gz == nz - 1)
+    def _():
+        F[:, :, S + BZ:NZE, :, :] = jnp.zeros((2, 2, S, ROWS, 128), jnp.float32)
+
+    @pl.when(yv == 0)
+    def _():
+        F[:, :, :, LO:MID, :] = jnp.zeros((2, 2, NZE, 8, 128), jnp.float32)
+
+    @pl.when(yv == nyv - 1)
+    def _():
+        F[:, :, :, HI:HI + 8, :] = jnp.zeros((2, 2, NZE, 8, 128), jnp.float32)
+
+    X[...] = jnp.zeros(X.shape, jnp.float32)
+
+    row = lax.broadcasted_iota(jnp.int32, (24, 128), 0) + (8 * yv - 8)
+    row_in = jnp.where((row >= 0) & (row < 8 * nyv), 2.0 / HALF, 0.0)
+    for z in range(NZE):
+        at = gz * BZ + (z - S)
+        M[z] = row_in * jnp.where((at >= 0) & (at < nz * BZ), 1.0, 0.0)
+
+    nz_near = jnp.where(gz > 0, 1, 0) + jnp.where(gz < nz - 1, 1, 0)
+    pl.semaphore_wait(barrier, len(plane) + len(line) + nz_near * jnp.where(has_off, 2, 1))
     swaps = []
-    for f, ref in enumerate((rhs_ref, diag_ref)):
+    for f in range(2):
+        loads[f].wait()
         cp = pltpu.make_async_remote_copy(
-            src_ref=ref.at[:, pl.ds(pl.multiple_of(8 * sib, 8), 8), :],
+            src_ref=land.at[f],
             dst_ref=F.at[f, gx, own_z, own_rows, :],
             send_sem=io_s.at[f], recv_sem=io_r.at[f],
             device_id=(gz, gy, sib), device_id_type=MESH,
         )
         cp.start()
         swaps.append(cp)
-        F[f, gx, S:S + BZ, MID:MID + 8, :] = ref[:, pl.ds(pl.multiple_of(8 * gx, 8), 8), :]
-
-    @pl.when(gz == 0)
-    def _():
-        F[:, :, 0:S, :, :] = jnp.zeros((2, 2, S, ROWS, 128), jnp.float32)
-
-    @pl.when(gz == nz - 1)
-    def _():
-        F[:, :, S + BZ:NZE, :, :] = jnp.zeros((2, 2, S, ROWS, 128), jnp.float32)
-
-    @pl.when(yv == 0)
-    def _():
-        F[:, :, :, LO:MID, :] = jnp.zeros((2, 2, NZE, 8, 128), jnp.float32)
-
-    @pl.when(yv == nyv - 1)
-    def _():
-        F[:, :, :, HI:HI + 8, :] = jnp.zeros((2, 2, NZE, 8, 128), jnp.float32)
-
-    X[...] = jnp.zeros(X.shape, jnp.float32)
-
-    row = lax.broadcasted_iota(jnp.int32, (24, 128), 0) + (8 * yv - 8)
-    row_in = jnp.where((row >= 0) & (row < 8 * nyv), 2.0 / HALF, 0.0)
-    for z in range(NZE):
-        at = gz * BZ + (z - S)
-        M[z] = row_in * jnp.where((at >= 0) & (at < nz * BZ), 1.0, 0.0)
-
-    for cp in swaps:
+    for cp in loads[2:] + swaps:
         cp.wait()
 
     lane = lax.broadcasted_iota(jnp.int32, (24, 128), 1)
@@ -133,71 +175,81 @@
         s1 = v[1] + jnp.where(first, a0, a1) + jnp.where(last, zero, b1)
         return s0, s1
 
-    def neighbours(dz=0, dy=0):
-        t = yv + dy
-        return (gz + dz, t // 2, t % 2)
+    off_rows = pl.ds(pl.multiple_of(LO + 16 * sib, 8), 8)
+    sib_rows = pl.ds(pl.multiple_of(LO + 16 * gx, 8), 8)
+    bands = (pl.ds(S + BZ, S), pl.ds(0, S))
+    edges = (pl.ds(S, S), pl.ds(BZ, S))
+    near = (gz - 1, gz + 1)
+
+    def remote(src_planes, dst_planes, dst_rows, send, recv, to):
+        return pltpu.make_async_remote_copy(
+            src_ref=F.at[:, :, src_planes, own_rows, :], dst_ref=F.at[:, :, dst_planes, dst_rows, :],
+            send_sem=send, recv_sem=recv, device_id=to, device_id_type=MESH,
+        )
 
     def z_copy(k):
-        src, dst, dz = ((S, S + BZ, -1), (BZ, 0, 1))[k]
-        return pltpu.make_async_remote_copy(
-            src_ref=F.at[:, :, pl.ds(src, S), own_rows, :],
-            dst_ref=F.at[:, :, pl.ds(dst, S), own_rows, :],
-            send_sem=zs_sem.at[k], recv_sem=zr_sem.at[k],
-            device_id=neighbours(dz=dz), device_id_type=MESH,
-        )
-
-    def y_copy(k, planes, send, recv):
-        dst, dy = ((HI, -1), (LO, 1))[k]
-        return pltpu.make_async_remote_copy(
-            src_ref=F.at[:, :, planes, own_rows, :],
-            dst_ref=F.at[:, :, planes, pl.ds(dst, 8), :],
-            send_sem=send, recv_sem=recv,
-            device_id=neighbours(dy=dy), device_id_type=MESH,
-        )
-
-    to_z = (gz > 0, gz < nz - 1)
-    from_z = (gz < nz - 1, gz > 0)
-    to_y = (yv > 0, yv < nyv - 1)
-    from_y = (yv < nyv - 1, yv > 0)
-    bands = (pl.ds(S + BZ, S), pl.ds(0, S))
-
-    def exchange():
+        return remote(edges[k], bands[k], own_rows, zs_sem.at[k], zr_sem.at[k], (near[k], gy, gx))
+
+    def corner(k):
+        return remote(edges[k], bands[k], off_rows, cs_sem.at[k], cr_sem.at[k], (near[k], off_gy, sib))
+
+    def forward(k):
+        return remote(bands[k], bands[k], sib_rows, fs_sem.at[k], fr_sem.at[k], (gz, gy, sib))
+
+    y_off = remote(own_z, own_z, off_rows, ys_sem.at[0], yr_sem.at[0], (gz, off_gy, sib))
+    y_sib = remote(own_z, own_z, sib_rows, ys_sem.at[1], yr_sem.at[1], (gz, gy, sib))
+
+    def exchange_start():
         for k in range(2):
             @pl.when(to_z[k])
             def _(k=k):
                 z_copy(k).start()
+
+        @pl.when(has_off)
+        def _():
+            y_off.start()
         for k in range(2):
-            @pl.when(to_y[k])
-            def _(k=k):
-                y_copy(k, own_z, ys_sem.at[k], yr_sem.at[k]).start()
-        for b in range(2):
-            @pl.when(from_z[b])
-            def _(b=b):
-                z_copy(b).wait_recv()
-                for k in range(2):
-                    @pl.when(to_y[k])
-                    def _(k=k):
-                        y_copy(k, bands[b], fs_sem.at[b, k], fr_sem.at[b, k]).start()
+            @pl.when(to_z[k] & has_off)
+            def _(k=k):
+                corner(k).start()
+        y_sib.start()
+
+    def exchange_finish():
         for k in range(2):
-            @pl.when(from_y[k])
-            def _(k=k):
-                y_copy(k, own_z, ys_sem.at[k], yr_sem.at[k]).wait_recv()
-                for b in range(2):
-                    @pl.when(from_z[b])
-                    def _(b=b):
-                        y_copy(k, bands[b], fs_sem.at[b, k], fr_sem.at[b, k]).wait_recv()
+            @pl.when(from_z[k])
+            def _(k=k):
+                z_copy(k).wait_recv()
+                forward(k).start()
+        y_sib.wait_recv()
+
+        @pl.when(has_off)
+        def _():
+            y_off.wait_recv()
+        for k in range(2):
+            @pl.when(from_z[k])
+            def _(k=k):
+                forward(k).wait_recv()
+
+            @pl.when(from_z[k] & has_off)
+            def _(k=k):
+                corner(k).wait_recv()
+        y_sib.wait_send()
+
+        @pl.when(has_off)
+        def _():
+            y_off.wait_send()
         for k in range(2):
             @pl.when(to_z[k])
             def _(k=k):
                 z_copy(k).wait_send()
 
-            @pl.when(to_y[k])
-            def _(k=k):
-                y_copy(k, own_z, ys_sem.at[k], yr_sem.at[k]).wait_send()
-                for b in range(2):
-                    @pl.when(from_z[b])
-                    def _(b=b):
-                        y_copy(k, bands[b], fs_sem.at[b, k], fr_sem.at[b, k]).wait_send()
+            @pl.when(to_z[k] & has_off)
+            def _(k=k):
+                corner(k).wait_send()
+
+            @pl.when(from_z[k])
+            def _(k=k):
+                forward(k).wait_send()
 
     def power_steps(read, write, degree, z0, z1, rows):
         r0, n = rows
@@ -266,9 +318,24 @@
     from_low = (by_row([0.0, HALF] + [0.5 * HALF] * (S - 1)), by_row([0.0, HALF] + [0.5 * HALF] * (S - 2)))
     from_high = (by_row([0.5 * HALF] * (S - 1)), by_row([0.5 * HALF] * (S - 2)))
 
+    def combine(c, xt):
+        total = None
+        for block in range(2):
+            for degree in range(S + 1 - block):
+                half, row = place(degree + block * (S + 1))
+                term = splat(c[half], row)[None] * own(block, degree, xt)
+                total = term if total is None else total + term
+        return total
+
     def outer(t, carry):
         par = t % 2
-        exchange()
+        exchange_start()
+
+        @pl.when(t > 0)
+        def _():
+            for xt in range(2):
+                X[xt] = X[xt] + combine([XC[h] for h in range(PARTS)], xt)
+        exchange_finish()
 
         @pl.when(t == 0)
         def _():
@@ -314,21 +381,16 @@
 
         me1 = 8 * py + yv
         S1[par, me1] = local
-        for dy in range(4):
-            for dx in range(4):
-                for dc in range(2):
-                    if dy or dx or dc:
-                        to = (((py + dy) % 4) * nzp + pz, (gy + dx) % 4, (gx + dc) % 2)
-                        pltpu.make_async_remote_copy(
-                            src_ref=S1.at[par, me1], dst_ref=S1.at[par, me1],
-                            send_sem=g1_s.at[par], recv_sem=g1_r.at[par],
-                            device_id=to, device_id_type=MESH,
-                        ).start()
+        for to in plane:
+            pltpu.make_async_remote_copy(
+                src_ref=S1.at[par, me1], dst_ref=S1.at[par, me1],
+                send_sem=g1_s.at[par], recv_sem=g1_r.at[par],
+                device_id=to, device_id_type=MESH,
+            ).start()
         whole1 = pltpu.make_async_copy(S1.at[par, pl.ds(0, 31)], S1.at[par, pl.ds(0, 31)], g1_r.at[par])
         whole1.wait()
         S2[par, pz] = jnp.sum(S1[par], axis=0)
-        for dz in range(1, nzp):
-            to = (py * nzp + (pz + dz) % nzp, gy, gx)
+        for to in line:
             pltpu.make_async_remote_copy(
                 src_ref=S2.at[par, pz], dst_ref=S2.at[par, pz],
                 send_sem=g2_s.at[par], recv_sem=g2_r.at[par],
@@ -345,7 +407,7 @@
             [
                 [
                     jnp.broadcast_to(jnp.sum(w_ref[which, j, half] * moments, axis=1, keepdims=True), (8, 128))
-                    for half in range(2)
+                    for half in range(PARTS)
                 ]
                 for j in range(columns)
             ]
@@ -353,9 +415,9 @@
         ]
 
         def form(which, v):
-            col = [splat(v[0], j) for j in range(S + 1)] + [splat(v[1], j) for j in range(S)]
+            col = [splat(v[place(j)[0]], place(j)[1]) for j in range(columns)]
             total = None
-            for half in range(2):
+            for half in range(PARTS):
                 terms = [table[which][j][half] * col[j] for j in range(columns)]
                 while len(terms) > 1:
                     terms = [
@@ -367,54 +429,55 @@
 
         unit = jnp.where(sub8 == 0, 1.0, 0.0)
         none = jnp.zeros((8, 128), jnp.float32)
-        p_c, r_c, x_c = [unit, none], [none, unit], [none, none]
+        p_c, r_c, x_c = ([unit] + [none] * (PARTS - 1), [none, unit] + [none] * (PARTS - 2), [none] * PARTS)
         norm = form(0, r_c)
         for step in range(S):
             q = [
                 diag_c[h] * p_c[h] + from_low[h] * pltpu.roll(p_c[h], 1, 0) + from_high[h] * pltpu.roll(p_c[h], 7, 0)
                 for h in range(2)
             ]
+            if PARTS == 3:
+                q.append(jnp.where(sub8 == 0, 0.5 * HALF * splat(p_c[0], 7), 0.0))
             length = norm / form(1, p_c)
-            x_c = [x_c[h] + length * p_c[h] for h in range(2)]
-            r_c = [r_c[h] - length * q[h] for h in range(2)]
-            norm_next = form(0, r_c)
+            r_next = [r_c[h] - length * q[h] for h in range(PARTS)]
+            norm_next = form(0, r_next)
             ratio = norm_next / norm
-            p_c = [r_c[h] + ratio * p_c[h] for h in range(2)]
-            norm = norm_next
-
-        def combine(c, xt):
-            total = None
-            for block in range(2):
-                for degree in range(S + 1 - block):
-                    term = splat(c[block], degree)[None] * own(block, degree, xt)
-                    total = term if total is None else total + term
-            return total
+            new = (
+                [x_c[h] + length * p_c[h] for h in range(PARTS)] + r_next
+                + [r_next[h] + ratio * p_c[h] for h in range(PARTS)] + [norm_next]
+            )
+            count = sum(inner > step for inner in INNER)
+            if count < len(INNER):
+                keep = jnp.full((8, 128), t, jnp.int32) < count
+                new = [jnp.where(keep, a, b) for a, b in zip(new, x_c + r_c + p_c + [norm])]
+            x_c, r_c, p_c, norm = new[:PARTS], new[PARTS:2 * PARTS], new[2 * PARTS:3 * PARTS], new[-1]
 
         for xt in range(2):
             F[0, xt, S:S + BZ, MID:MID + 8, :] = combine(p_c, xt)
             F[1, xt, S:S + BZ, MID:MID + 8, :] = combine(r_c, xt)
-            X[xt] = X[xt] + combine(x_c, xt)
+        for h in range(PARTS):
+            XC[h] = x_c[h]
         return carry
 
-    lax.fori_loop(0, OUTER, outer, 0)
-
-    backs = []
-    for f, (src, out) in enumerate(
-        ((X.at[sib], sol_ref), (F.at[1, sib, own_z, own_rows, :], res_ref))
-    ):
-        cp = pltpu.make_async_remote_copy(
+    lax.fori_loop(0, len(INNER), outer, 0)
+
+    def back(f, src):
+        return pltpu.make_async_remote_copy(
             src_ref=src, dst_ref=land.at[f],
             send_sem=io_s.at[2 + f], recv_sem=io_r.at[2 + f],
             device_id=(gz, gy, sib), device_id_type=MESH,
         )
-        cp.start()
-        backs.append(cp)
-    mine = pl.ds(pl.multiple_of(8 * gx, 8), 8)
+
+    res_back = back(1, F.at[1, sib, own_z, own_rows, :])
+    res_back.start()
+    for xt in range(2):
+        X[xt] = X[xt] + combine([XC[h] for h in range(PARTS)], xt)
+    sol_back = back(0, X.at[sib])
+    sol_back.start()
+    res_ref[:, mine, :] = F[1, gx, S:S + BZ, MID:MID + 8, :]
     sol_ref[:, mine, :] = X[gx]
-    res_ref[:, mine, :] = F[1, gx, S:S + BZ, MID:MID + 8, :]
-    other = pl.ds(pl.multiple_of(8 * sib, 8), 8)
-    for f, out in enumerate((sol_ref, res_ref)):
-        backs[f].wait()
+    for f, (cp, out) in enumerate(((sol_back, sol_ref), (res_back, res_ref))):
+        cp.wait()
         out[:, other, :] = land[f]
 
 
@@ -428,7 +491,7 @@
         return pl.pallas_call(
             kernel,
             out_shape=(jax.ShapeDtypeStruct(right_side.shape, f32),) * 2,
-            in_specs=[pl.BlockSpec(memory_space=pltpu.VMEM)] * 3,
+            in_specs=[pl.BlockSpec(memory_space=pltpu.HBM)] * 3,
             out_specs=(pl.BlockSpec(memory_space=pltpu.VMEM),) * 2,
             scratch_shapes=[
                 pltpu.VMEM((2,) + field, f32),
@@ -438,13 +501,15 @@
                 pltpu.VMEM((NZE, 24, 128), f32),
                 pltpu.VMEM((2, 2, BZ, 8, 128), f32),
                 pltpu.VMEM((2, BZ, 8, 128), f32),
+                pltpu.VMEM((PARTS, 8, 128), f32),
                 pltpu.VMEM((2, BZ, 8, 128), f32),
                 pltpu.VMEM((2, 32, 1, 128), f32),
                 pltpu.VMEM((2, 8, 1, 128), f32),
-                dma((2,)), dma((2,)), dma((2,)), dma((2,)), dma((2, 2)), dma((2, 2)),
+                pltpu.VMEM(table.shape, f32),
+                dma((5,)), dma((2,)), dma((2,)), dma((2,)), dma((2,)), dma((2,)), dma((2,)), dma((2,)), dma((2,)),
                 dma((4,)), dma((4,)), dma((2,)), dma((2,)), dma((2,)), dma((2,)),
             ],
-            compiler_params=pltpu.CompilerParams(has_side_effects=True, vmem_limit_bytes=48 * 2**20),
+            compiler_params=pltpu.CompilerParams(collective_id=0, has_side_effects=True, vmem_limit_bytes=67043328),
         )(right_side, diagonal, jnp.asarray(table))
 
     spec = P("gz", "gy", "gx")

time: 125 us -> 107 us (0.86)
  Pallas kernels: 121 us -> 104 us
  local copies, waits for them, and re-layouts: 3.87 us -> 2.14 us
    pallas_call x1, Pallas kernels: 121 us -> 104 us  [local(): pl.pallas_call(kernel, out_shape=(jax.ShapeDtypeStruct(right_side.shape,...]
    unnamed x8 -> x4, local copies, waits for them, and re-layouts: 3.87 us -> 2.14 us
where the time goes in v2:
time: 107 us
  Pallas kernels  104 us (97%)
  local copies, waits for them, and re-layouts  2.14 us (2%)
    pallas_call x1, Pallas kernels, local(): pl.pallas_call(kernel, out_shape=(jax.ShapeDtypeStruct(right_side.shape,...  104 us

profile of v2, /device:TPU:1, one launch (start us, length us, event | category | flops | bytes accessed | tf_op | source)
XLA Modules:
  0.0 106.8 jit_solution(631898587604964762)
XLA Ops:
  0.6 104.0 %shard_map.50 = (f32[8,16,128]{2,1,0:T(8,128)}, f32[8,16,128]{2,1,0:T(8,128)}) custom-call(f32[8,16,128]{2,1,0:T(8,128)} %rhs_ref.1, f32[8,16,128]{2,1,0:T(8,128)} %diag_ref.1, f32[2,13,2,8,128]{4,3,2,1,0:T(8,128)} %constant.2.clone.w_hbm), custom_call_target="tpu_custom_call" | custom-call | tf_op jit(solution)/shard_map/pallas_call | solution.py:491
  104.7 0.0 copy-start
  104.7 1.5 %copy.7 = f32[8,16,128]{2,1,0:T(8,128)} copy(f32[8,16,128]{2,1,0:T(8,128)} %get-tuple-element.4) | data formatting | bytes 131072
  106.2 0.0 copy-done
  106.2 0.6 copy.8
Async XLA Ops:
  104.7 1.5 %copy-start = (f32[8,16,128]{2,1,0:T(8,128)S(1)}, f32[8,16,128]{2,1,0:T(8,128)}, u32[]{:S(2)}) copy-start(f32[8,16,128]{2,1,0:T(8,128)} %get-tuple-element.5) | copy-start | bytes 196612

commit v3 on v2

--- a/solution.py
+++ b/solution.py
@@ -8,8 +8,8 @@
 from jax.experimental.pallas import tpu as pltpu
 from jax.sharding import PartitionSpec as P
 
-S = 6
-INNER = (6,) * 5
+S = 8
+INNER = (8, 8, 7, 7)
 MESH = pl.DeviceIdType.MESH
 
 CENTER = 19.0

time: 107 us -> 99.9 us (0.934)
  Pallas kernels: 104 us -> 97 us
    pallas_call x1, Pallas kernels: 104 us -> 97 us  [local(): pl.pallas_call(kernel, out_shape=(jax.ShapeDtypeStruct(right_side.shape,...]
where the time goes in v3:
time: 99.9 us; the launch traced here: 99.8 us
  Pallas kernels  97 us (97%)
  local copies, waits for them, and re-layouts  2.14 us (2%)
    pallas_call x1, Pallas kernels, local(): pl.pallas_call(kernel, out_shape=(jax.ShapeDtypeStruct(right_side.shape,...  97 us
    unnamed x4, local copies, waits for them, and re-layouts  2.14 us

profile of v3, /device:TPU:1, one launch (start us, length us, event | category | flops | bytes accessed | tf_op | source)
XLA Modules:
  0.0 99.8 jit_solution(10720369017079935863)
XLA Ops:
  0.6 97.0 %shard_map.50 = (f32[8,16,128]{2,1,0:T(8,128)}, f32[8,16,128]{2,1,0:T(8,128)}) custom-call(f32[8,16,128]{2,1,0:T(8,128)} %rhs_ref.1, f32[8,16,128]{2,1,0:T(8,128)} %diag_ref.1, f32[2,17,3,8,128]{4,3,2,1,0:T(8,128)} %constant.2.clone.w_hbm), custom_call_target="tpu_custom_call" | custom-call | tf_op jit(solution)/shard_map/pallas_call | solution.py:491
  97.6 0.0 copy-start
  97.6 1.5 %copy.7 = f32[8,16,128]{2,1,0:T(8,128)} copy(f32[8,16,128]{2,1,0:T(8,128)} %get-tuple-element.4) | data formatting | bytes 131072
  99.1 0.0 copy-done
  99.1 0.6 copy.8
Async XLA Ops:
  97.6 1.5 %copy-start = (f32[8,16,128]{2,1,0:T(8,128)S(1)}, f32[8,16,128]{2,1,0:T(8,128)}, u32[]{:S(2)}) copy-start(f32[8,16,128]{2,1,0:T(8,128)} %get-tuple-element.5) | copy-start | bytes 196612

commit v4 on v3

--- a/solution.py
+++ b/solution.py
@@ -51,22 +51,11 @@
             kinds = (i > S) + (j > S)
             offset = (0, NPP, NPP + NPR)[kinds]
             gram[i, j] = (moment(offset, di + dj) + moment(offset, abs(di - dj))) / 2
-    change = np.zeros((columns, columns))
-    for offset, length in ((0, S), (S + 1, S - 1)):
-        for degree in range(length):
-            change[offset + degree, offset + degree] = CENTER
-            if degree == 0:
-                change[offset + 1, offset] = HALF
-            else:
-                change[offset + degree + 1, offset + degree] = 0.5 * HALF
-                change[offset + degree - 1, offset + degree] = 0.5 * HALF
-    moved = np.einsum("ikm,kj->ijm", gram, change)
-    out = np.zeros((2, columns, PARTS, 8, 128), np.float32)
-    for which, table in enumerate((gram, moved)):
-        for j in range(columns):
-            for i in range(columns):
-                half, row = place(i)
-                out[which, j, half, row, :total] = table[i, j]
+    out = np.zeros((columns, PARTS, 8, 128), np.float32)
+    for j in range(columns):
+        for i in range(columns):
+            half, row = place(i)
+            out[j, half, row, :total] = gram[i, j]
     return out
 
 
@@ -303,6 +292,17 @@
         v = v + pltpu.roll(v, 4, 0)
         v = v + pltpu.roll(v, 2, 0)
         return v + pltpu.roll(v, 1, 0)
+
+    def exact_sum(pairs):
+        while len(pairs) > 1:
+            joined = []
+            for (a, ea), (b, eb) in zip(pairs[::2], pairs[1::2]):
+                t = a + b
+                back = t - a
+                err = (a - (t - back)) + (b - back)
+                joined.append((t, err if ea is None else err + (ea + eb)))
+            pairs = joined
+        return pairs[0]
 
     def splat(v, j):
         return jnp.broadcast_to(v[j:j + 1, :], (8, 128))
@@ -389,7 +389,7 @@
             ).start()
         whole1 = pltpu.make_async_copy(S1.at[par, pl.ds(0, 31)], S1.at[par, pl.ds(0, 31)], g1_r.at[par])
         whole1.wait()
-        S2[par, pz] = jnp.sum(S1[par], axis=0)
+        S2[par, pz] = jnp.concatenate(exact_sum([(S1[par, i], None) for i in range(32)]), axis=0)
         for to in line:
             pltpu.make_async_remote_copy(
                 src_ref=S2.at[par, pz], dst_ref=S2.at[par, pz],
@@ -398,39 +398,40 @@
             ).start()
         whole2 = pltpu.make_async_copy(S2.at[par, pl.ds(0, 7)], S2.at[par, pl.ds(0, 7)], g2_r.at[par])
         whole2.wait()
-        moments = jnp.broadcast_to(jnp.sum(S2[par], axis=0), (8, 128))
+        high, low = exact_sum([(S2[par, i, 0:1], S2[par, i, 1:2]) for i in range(nzp)])
+        lead = high.astype(jnp.bfloat16).astype(jnp.float32)
+        rest = (high - lead) + low
+        lead, rest = jnp.broadcast_to(lead, (8, 128)), jnp.broadcast_to(rest, (8, 128))
         pltpu.make_async_copy(S1.at[par, pl.ds(0, 31)], S1.at[par, pl.ds(0, 31)], g1_s.at[par]).wait()
         pltpu.make_async_copy(S2.at[par, pl.ds(0, 7)], S2.at[par, pl.ds(0, 7)], g2_s.at[par]).wait()
 
         columns = 2 * S + 1
+
+        def lanes(v):
+            return jnp.broadcast_to(jnp.sum(v, axis=1, keepdims=True), (8, 128))
+
         table = [
-            [
-                [
-                    jnp.broadcast_to(jnp.sum(w_ref[which, j, half] * moments, axis=1, keepdims=True), (8, 128))
-                    for half in range(PARTS)
-                ]
-                for j in range(columns)
-            ]
-            for which in range(2)
+            [lanes(w_ref[j, half] * lead) + lanes(w_ref[j, half] * rest) for half in range(PARTS)]
+            for j in range(columns)
         ]
 
-        def form(which, v):
+        def form(u, v):
             col = [splat(v[place(j)[0]], place(j)[1]) for j in range(columns)]
             total = None
             for half in range(PARTS):
-                terms = [table[which][j][half] * col[j] for j in range(columns)]
+                terms = [table[j][half] * col[j] for j in range(columns)]
                 while len(terms) > 1:
                     terms = [
                         terms[i] + terms[i + 1] if i + 1 < len(terms) else terms[i] for i in range(0, len(terms), 2)
                     ]
-                part = terms[0] * v[half]
+                part = terms[0] * u[half]
                 total = part if total is None else total + part
             return all_sublanes(total)
 
         unit = jnp.where(sub8 == 0, 1.0, 0.0)
         none = jnp.zeros((8, 128), jnp.float32)
         p_c, r_c, x_c = ([unit] + [none] * (PARTS - 1), [none, unit] + [none] * (PARTS - 2), [none] * PARTS)
-        norm = form(0, r_c)
+        norm = form(r_c, r_c)
         for step in range(S):
             q = [
                 diag_c[h] * p_c[h] + from_low[h] * pltpu.roll(p_c[h], 1, 0) + from_high[h] * pltpu.roll(p_c[h], 7, 0)
@@ -438,9 +439,9 @@
             ]
             if PARTS == 3:
                 q.append(jnp.where(sub8 == 0, 0.5 * HALF * splat(p_c[0], 7), 0.0))
-            length = norm / form(1, p_c)
+            length = norm / form(p_c, q)
             r_next = [r_c[h] - length * q[h] for h in range(PARTS)]
-            norm_next = form(0, r_next)
+            norm_next = form(r_next, r_next)
             ratio = norm_next / norm
             new = (
                 [x_c[h] + length * p_c[h] for h in range(PARTS)] + r_next
@@ -504,7 +505,7 @@
                 pltpu.VMEM((PARTS, 8, 128), f32),
                 pltpu.VMEM((2, BZ, 8, 128), f32),
                 pltpu.VMEM((2, 32, 1, 128), f32),
-                pltpu.VMEM((2, 8, 1, 128), f32),
+                pltpu.VMEM((2, 8, 2, 128), f32),
                 pltpu.VMEM(table.shape, f32),
                 dma((5,)), dma((2,)), dma((2,)), dma((2,)), dma((2,)), dma((2,)), dma((2,)), dma((2,)), dma((2,)),
                 dma((4,)), dma((4,)), dma((2,)), dma((2,)), dma((2,)), dma((2,)),

time: 99.9 us -> 100 us (level)
  no operation moved by 1% of the time
where the time goes in v4:
time: 100 us; the launch traced here: 99.9 us
  Pallas kernels  97.2 us (97%)
  local copies, waits for them, and re-layouts  2.14 us (2%)
    pallas_call x1, Pallas kernels, local(): pl.pallas_call(kernel, out_shape=(jax.ShapeDtypeStruct(right_side.shape,...  97.2 us
    unnamed x4, local copies, waits for them, and re-layouts  2.14 us

profile of v4, /device:TPU:1, one launch (start us, length us, event | category | flops | bytes accessed | tf_op | source)
XLA Modules:
  0.0 99.9 jit_solution(16329572675531626836)
XLA Ops:
  0.6 97.2 %shard_map.50 = (f32[8,16,128]{2,1,0:T(8,128)}, f32[8,16,128]{2,1,0:T(8,128)}) custom-call(f32[8,16,128]{2,1,0:T(8,128)} %rhs_ref.1, f32[8,16,128]{2,1,0:T(8,128)} %diag_ref.1, f32[17,3,8,128]{3,2,1,0:T(8,128)} %constant.2.clone.w_hbm), custom_call_target="tpu_custom_call" | custom-call | tf_op jit(solution)/shard_map/pallas_call | solution.py:492
  97.8 0.0 copy-start
  97.8 1.5 %copy.7 = f32[8,16,128]{2,1,0:T(8,128)} copy(f32[8,16,128]{2,1,0:T(8,128)} %get-tuple-element.4) | data formatting | bytes 131072
  99.3 0.0 copy-done
  99.3 0.6 copy.8
Async XLA Ops:
  97.8 1.5 %copy-start = (f32[8,16,128]{2,1,0:T(8,128)S(1)}, f32[8,16,128]{2,1,0:T(8,128)}, u32[]{:S(2)}) copy-start(f32[8,16,128]{2,1,0:T(8,128)} %get-tuple-element.5) | copy-start | bytes 196612

commit v5 on v4

--- a/solution.py
+++ b/solution.py
@@ -166,79 +166,104 @@
 
     off_rows = pl.ds(pl.multiple_of(LO + 16 * sib, 8), 8)
     sib_rows = pl.ds(pl.multiple_of(LO + 16 * gx, 8), 8)
-    bands = (pl.ds(S + BZ, S), pl.ds(0, S))
-    edges = (pl.ds(S, S), pl.ds(BZ, S))
     near = (gz - 1, gz + 1)
 
-    def remote(src_planes, dst_planes, dst_rows, send, recv, to):
+    def bands(k, f):
+        return (pl.ds(S + BZ, S - f), pl.ds(f, S - f))[k]
+
+    def edges(k, f):
+        return (pl.ds(S, S - f), pl.ds(BZ + f, S - f))[k]
+
+    def remote(f, src_planes, dst_planes, dst_rows, send, recv, to):
         return pltpu.make_async_remote_copy(
-            src_ref=F.at[:, :, src_planes, own_rows, :], dst_ref=F.at[:, :, dst_planes, dst_rows, :],
+            src_ref=F.at[f, :, src_planes, own_rows, :], dst_ref=F.at[f, :, dst_planes, dst_rows, :],
             send_sem=send, recv_sem=recv, device_id=to, device_id_type=MESH,
         )
 
-    def z_copy(k):
-        return remote(edges[k], bands[k], own_rows, zs_sem.at[k], zr_sem.at[k], (near[k], gy, gx))
-
-    def corner(k):
-        return remote(edges[k], bands[k], off_rows, cs_sem.at[k], cr_sem.at[k], (near[k], off_gy, sib))
-
-    def forward(k):
-        return remote(bands[k], bands[k], sib_rows, fs_sem.at[k], fr_sem.at[k], (gz, gy, sib))
-
-    y_off = remote(own_z, own_z, off_rows, ys_sem.at[0], yr_sem.at[0], (gz, off_gy, sib))
-    y_sib = remote(own_z, own_z, sib_rows, ys_sem.at[1], yr_sem.at[1], (gz, gy, sib))
+    def z_copy(k, f):
+        return remote(f, edges(k, f), bands(k, f), own_rows, zs_sem.at[k, f], zr_sem.at[k, f], (near[k], gy, gx))
+
+    def corner(k, f):
+        return remote(
+            f, edges(k, f), bands(k, f), off_rows, cs_sem.at[k, f], cr_sem.at[k, f], (near[k], off_gy, sib)
+        )
+
+    def forward(k, f):
+        return remote(f, bands(k, f), bands(k, f), sib_rows, fs_sem.at[k, f], fr_sem.at[k, f], (gz, gy, sib))
+
+    def y_off(f):
+        return remote(f, own_z, own_z, off_rows, ys_sem.at[0, f], yr_sem.at[0, f], (gz, off_gy, sib))
+
+    def y_sib(f):
+        return remote(f, own_z, own_z, sib_rows, ys_sem.at[1, f], yr_sem.at[1, f], (gz, gy, sib))
 
     def exchange_start():
         for k in range(2):
             @pl.when(to_z[k])
             def _(k=k):
-                z_copy(k).start()
+                for f in range(2):
+                    z_copy(k, f).start()
 
         @pl.when(has_off)
         def _():
-            y_off.start()
+            for f in range(2):
+                y_off(f).start()
         for k in range(2):
             @pl.when(to_z[k] & has_off)
             def _(k=k):
-                corner(k).start()
-        y_sib.start()
+                for f in range(2):
+                    corner(k, f).start()
+        for f in range(2):
+            y_sib(f).start()
 
     def exchange_finish():
+        for f in range(2):
+            for k in range(2):
+                @pl.when(from_z[k])
+                def _(k=k, f=f):
+                    z_copy(k, f).wait_recv()
+                    forward(k, f).start()
+        for f in range(2):
+            y_sib(f).wait_recv()
+
+        @pl.when(has_off)
+        def _():
+            for f in range(2):
+                y_off(f).wait_recv()
         for k in range(2):
             @pl.when(from_z[k])
             def _(k=k):
-                z_copy(k).wait_recv()
-                forward(k).start()
-        y_sib.wait_recv()
+                for f in range(2):
+                    forward(k, f).wait_recv()
+
+            @pl.when(from_z[k] & has_off)
+            def _(k=k):
+                for f in range(2):
+                    corner(k, f).wait_recv()
+
+    def exchange_sent():
+        for f in range(2):
+            y_sib(f).wait_send()
 
         @pl.when(has_off)
         def _():
-            y_off.wait_recv()
-        for k in range(2):
-            @pl.when(from_z[k])
-            def _(k=k):
-                forward(k).wait_recv()
-
-            @pl.when(from_z[k] & has_off)
-            def _(k=k):
-                corner(k).wait_recv()
-        y_sib.wait_send()
-
-        @pl.when(has_off)
-        def _():
-            y_off.wait_send()
+            for f in range(2):
+                y_off(f).wait_send()
         for k in range(2):
             @pl.when(to_z[k])
             def _(k=k):
-                z_copy(k).wait_send()
+                for f in range(2):
+                    z_copy(k, f).wait_send()
 
             @pl.when(to_z[k] & has_off)
             def _(k=k):
-                corner(k).wait_send()
+                for f in range(2):
+                    corner(k, f).wait_send()
 
             @pl.when(from_z[k])
             def _(k=k):
-                forward(k).wait_send()
+                for f in range(2):
+                    forward(k, f).wait_send()
 
     def power_steps(read, write, degree, z0, z1, rows):
         r0, n = rows
@@ -339,6 +364,7 @@
 
         @pl.when(t == 0)
         def _():
+            exchange_sent()
             for z in range(NZE):
                 C[:, z, LO:HI + 8, :] = (2.0 / HALF) * (
                     F[1, :, z, LO:HI + 8, :] + (27.0 - CENTER)
@@ -347,12 +373,13 @@
 
         for f in range(2):
             V0[f] = F[f, :, S:S + BZ, MID:MID + 8, :]
+        def window(margin):
+            return (LO, 24) if margin > 4 else (MID - 4, 16) if margin else (MID, 8)
+
         for degree in range(1, S + 1):
-            rows = (LO, 24) if degree < S else (MID, 8)
-            power_steps(read_p, write_p, degree, degree, NZE - degree, rows)
+            power_steps(read_p, write_p, degree, degree, NZE - degree, window(S - degree))
             if degree < S:
-                rows = (LO, 24) if degree < S - 1 else (MID, 8)
-                power_steps(read_r, write_r, degree, degree + 1, NZE - degree - 1, rows)
+                power_steps(read_r, write_r, degree, degree + 1, NZE - degree - 1, window(S - 1 - degree))
 
         parts = [None] * (NPP + NPR + NRR)
 
@@ -380,6 +407,9 @@
         local = jnp.sum(picked, axis=0, keepdims=True)
 
         me1 = 8 * py + yv
+        @pl.when(t > 0)
+        def _():
+            exchange_sent()
         S1[par, me1] = local
         for to in plane:
             pltpu.make_async_remote_copy(
@@ -507,11 +537,11 @@
                 pltpu.VMEM((2, 32, 1, 128), f32),
                 pltpu.VMEM((2, 8, 2, 128), f32),
                 pltpu.VMEM(table.shape, f32),
-                dma((5,)), dma((2,)), dma((2,)), dma((2,)), dma((2,)), dma((2,)), dma((2,)), dma((2,)), dma((2,)),
+                dma((5,)), dma((2, 2)), dma((2, 2)), dma((2, 2)), dma((2, 2)), dma((2, 2)), dma((2, 2)), dma((2, 2)), dma((2, 2)),
                 dma((4,)), dma((4,)), dma((2,)), dma((2,)), dma((2,)), dma((2,)),
             ],
-            compiler_params=pltpu.CompilerParams(collective_id=0, has_side_effects=True, vmem_limit_bytes=67043328),
-        )(right_side, diagonal, jnp.asarray(table))
+            compiler_params=pltpu.CompilerParams(collective_id=0, has_side_effects=True, vmem_limit_bytes=48 * 2**20),
+        )(*(pltpu.with_memory_space_constraint(v, pltpu.HBM) for v in (right_side, diagonal, jnp.asarray(table))))
 
     spec = P("gz", "gy", "gx")
     return jax.shard_map(

time: 100 us -> 95.5 us (0.955)
  Pallas kernels: 97.2 us -> 93.5 us
    pallas_call x1, Pallas kernels: 97.2 us -> 93.5 us  [local(): pl.pallas_call(kernel, out_shape=(jax.ShapeDtypeStruct(right_side.shape,...]
    unnamed x4 -> x2, local copies, waits for them, and re-layouts: 2.14 us -> 1.26 us
where the time goes in v5:
time: 95.5 us; the launch traced here: 95.4 us
  Pallas kernels  93.5 us (98%)
  local copies, waits for them, and re-layouts  1.26 us (1%)
    pallas_call x1, Pallas kernels, local(): pl.pallas_call(kernel, out_shape=(jax.ShapeDtypeStruct(right_side.shape,...  93.5 us

profile of v5, /device:TPU:1, one launch (start us, length us, event | category | flops | bytes accessed | tf_op | source)
XLA Modules:
  0.0 95.4 jit_solution(7384933487282702630)
XLA Ops:
  0.6 93.5 %shard_map.50 = (f32[8,16,128]{2,1,0:T(8,128)S(1)}, f32[8,16,128]{2,1,0:T(8,128)S(1)}) custom-call(f32[8,16,128]{2,1,0:T(8,128)} %rhs_ref.1, f32[8,16,128]{2,1,0:T(8,128)} %diag_ref.1, f32[17,3,8,128]{3,2,1,0:T(8,128)} %constant.2.clone.w_hbm), custom_call_target="tpu_custom_call" | custom-call | tf_op jit(solution)/shard_map/pallas_call | solution.py:522
  94.2 0.6 copy.7
  94.8 0.6 copy.8

commit v6 on v5

--- a/solution.py
+++ b/solution.py
@@ -155,14 +155,25 @@
     lane = lax.broadcasted_iota(jnp.int32, (24, 128), 1)
 
     def x_sum(v, rows):
-        first = lane[:rows] == 0
-        last = lane[:rows] == 127
-        a0, a1 = pltpu.roll(v[0], 1, 1), pltpu.roll(v[1], 1, 1)
-        b0, b1 = pltpu.roll(v[0], 127, 1), pltpu.roll(v[1], 127, 1)
-        zero = jnp.zeros((rows, 128), jnp.float32)
-        s0 = v[0] + jnp.where(first, zero, a0) + jnp.where(last, b1, b0)
-        s1 = v[1] + jnp.where(first, a0, a1) + jnp.where(last, zero, b1)
+        both = v[0] + v[1]
+        s0 = both + jnp.where(lane[:rows] == 0, 0.0, pltpu.roll(v[1], 1, 1))
+        s1 = both + jnp.where(lane[:rows] == 127, 0.0, pltpu.roll(v[0], 127, 1))
         return s0, s1
+
+    def reorder(pair, order):
+        n = pair[0].shape[0]
+        wide = jnp.concatenate([pair[0].reshape(8 * n, 128), pair[1].reshape(8 * n, 128)], axis=1)
+        out = jnp.dot(wide, order, precision=lax.Precision.HIGHEST, preferred_element_type=jnp.float32)
+        return [out[:, 128 * h:128 * (h + 1)].reshape(n, 8, 128) for h in range(2)]
+
+    at_i = lax.broadcasted_iota(jnp.int32, (256, 256), 0)
+    at_j = lax.broadcasted_iota(jnp.int32, (256, 256), 1)
+    to_stored = jnp.where(at_i == 2 * (at_j & 127) + (at_j >> 7), 1.0, 0.0)
+    to_natural = jnp.where(at_j == 2 * (at_i & 127) + (at_i >> 7), 1.0, 0.0)
+    for f in range(2):
+        halves = reorder(F[f, :, S:S + BZ, MID:MID + 8, :], to_stored)
+        for xt in range(2):
+            F[f, xt, S:S + BZ, MID:MID + 8, :] = halves[xt]
 
     off_rows = pl.ds(pl.multiple_of(LO + 16 * sib, 8), 8)
     sib_rows = pl.ds(pl.multiple_of(LO + 16 * gx, 8), 8)
@@ -277,8 +288,14 @@
                 )
             return sums[z]
 
+        shared = None
         for z in range(z0, z1):
-            s0, s1 = x_sum(y_sum(z - 1) + y_sum(z) + y_sum(z + 1), n)
+            if shared is None:
+                shared = y_sum(z) + y_sum(z + 1)
+                s0, s1 = x_sum(shared + y_sum(z - 1), n)
+            else:
+                s0, s1 = x_sum(shared + y_sum(z + 1), n)
+                shared = None
             sums.pop(z - 1, None)
             mask = M[z, m0:m0 + n, :]
             box = jnp.stack([s0 * mask, s1 * mask])
@@ -499,10 +516,14 @@
             device_id=(gz, gy, sib), device_id_type=MESH,
         )
 
+    halves = reorder(F[1, :, S:S + BZ, MID:MID + 8, :], to_natural)
+    for xt in range(2):
+        F[1, xt, S:S + BZ, MID:MID + 8, :] = halves[xt]
     res_back = back(1, F.at[1, sib, own_z, own_rows, :])
     res_back.start()
+    halves = reorder([X[xt] + combine([XC[h] for h in range(PARTS)], xt) for xt in range(2)], to_natural)
     for xt in range(2):
-        X[xt] = X[xt] + combine([XC[h] for h in range(PARTS)], xt)
+        X[xt] = halves[xt]
     sol_back = back(0, X.at[sib])
     sol_back.start()
     res_ref[:, mine, :] = F[1, gx, S:S + BZ, MID:MID + 8, :]

time: 95.5 us -> 94.6 us (level)
  no operation moved by 1% of the time
where the time goes in v6:
time: 94.6 us; the launch traced here: 94.5 us
  Pallas kernels  92.6 us (98%)
  local copies, waits for them, and re-layouts  1.26 us (1%)
    pallas_call x1, Pallas kernels, local(): pl.pallas_call(kernel, out_shape=(jax.ShapeDtypeStruct(right_side.shape,...  92.6 us

profile of v6, /device:TPU:1, one launch (start us, length us, event | category | flops | bytes accessed | tf_op | source)
XLA Modules:
  0.0 94.5 jit_solution(1674512777511976284)
XLA Ops:
  0.6 92.6 %shard_map.50 = (f32[8,16,128]{2,1,0:T(8,128)S(1)}, f32[8,16,128]{2,1,0:T(8,128)S(1)}) custom-call(f32[8,16,128]{2,1,0:T(8,128)} %rhs_ref.1, f32[8,16,128]{2,1,0:T(8,128)} %diag_ref.1, f32[17,3,8,128]{3,2,1,0:T(8,128)} %constant.2.clone.w_hbm), custom_call_target="tpu_custom_call" | custom-call | tf_op jit(solution)/shard_map/pallas_call | solution.py:543
  93.3 0.6 copy.7
  93.9 0.6 copy.8

commit v7 on v6

--- a/solution.py
+++ b/solution.py
@@ -130,7 +130,7 @@
 
     X[...] = jnp.zeros(X.shape, jnp.float32)
 
-    row = lax.broadcasted_iota(jnp.int32, (24, 128), 0) + (8 * yv - 8)
+    row = lax.broadcasted_iota(jnp.int32, (ROWS, 128), 0) + (8 * yv - MID)
     row_in = jnp.where((row >= 0) & (row < 8 * nyv), 2.0 / HALF, 0.0)
     for z in range(NZE):
         at = gz * BZ + (z - S)
@@ -236,17 +236,18 @@
                     forward(k, f).start()
         for f in range(2):
             y_sib(f).wait_recv()
-
+        for k in range(2):
+            @pl.when(from_z[k])
+            def _(k=k):
+                for f in range(2):
+                    forward(k, f).wait_recv()
+
+    def exchange_last():
         @pl.when(has_off)
         def _():
             for f in range(2):
                 y_off(f).wait_recv()
         for k in range(2):
-            @pl.when(from_z[k])
-            def _(k=k):
-                for f in range(2):
-                    forward(k, f).wait_recv()
-
             @pl.when(from_z[k] & has_off)
             def _(k=k):
                 for f in range(2):
@@ -278,7 +279,6 @@
 
     def power_steps(read, write, degree, z0, z1, rows):
         r0, n = rows
-        m0 = r0 - LO
         sums = {}
 
         def y_sum(z):
@@ -297,7 +297,7 @@
                 s0, s1 = x_sum(shared + y_sum(z + 1), n)
                 shared = None
             sums.pop(z - 1, None)
-            mask = M[z, m0:m0 + n, :]
+            mask = M[z, r0:r0 + n, :]
             box = jnp.stack([s0 * mask, s1 * mask])
             value = C[:, z, r0:r0 + n, :] * read(degree - 1, z, r0, n) - box
             if degree == 1:
@@ -381,6 +381,7 @@
 
         @pl.when(t == 0)
         def _():
+            exchange_last()
             exchange_sent()
             for z in range(NZE):
                 C[:, z, LO:HI + 8, :] = (2.0 / HALF) * (
@@ -390,13 +391,29 @@
 
         for f in range(2):
             V0[f] = F[f, :, S:S + BZ, MID:MID + 8, :]
-        def window(margin):
-            return (LO, 24) if margin > 4 else (MID - 4, 16) if margin else (MID, 8)
-
-        for degree in range(1, S + 1):
-            power_steps(read_p, write_p, degree, degree, NZE - degree, window(S - degree))
-            if degree < S:
-                power_steps(read_r, write_r, degree, degree + 1, NZE - degree - 1, window(S - 1 - degree))
+        def early_rows(core, m):
+            n = 8 * ((2 * m + 7) // 8)
+            return (MID + m - n if core else MID + 8 - m, n)
+
+        def late_rows(core, m):
+            return (MID + m if core else MID - m, 8)
+
+        def powers(rows, core):
+            for degree in range(1, S + 1):
+                for f, (read, write) in enumerate(((read_p, write_p), (read_r, write_r))):
+                    m = S - f - degree
+                    if m >= 0 and rows(core, m)[1]:
+                        power_steps(read, write, degree, degree + f, NZE - degree - f, rows(core, m))
+
+        for core in range(2):
+            @pl.when(gx == core)
+            def _(core=core):
+                powers(early_rows, core)
+
+                @pl.when(t > 0)
+                def _():
+                    exchange_last()
+                powers(late_rows, core)
 
         parts = [None] * (NPP + NPR + NRR)
 
@@ -462,11 +479,11 @@
             for j in range(columns)
         ]
 
-        def form(u, v):
-            col = [splat(v[place(j)[0]], place(j)[1]) for j in range(columns)]
+        def form(u, v, top_p, top_r):
+            used = list(range(top_p + 1)) + [S + 1 + j for j in range(top_r + 1)]
             total = None
-            for half in range(PARTS):
-                terms = [table[j][half] * col[j] for j in range(columns)]
+            for half in sorted({place(j)[0] for j in used}):
+                terms = [table[j][half] * splat(v[place(j)[0]], place(j)[1]) for j in used]
                 while len(terms) > 1:
                     terms = [
                         terms[i] + terms[i + 1] if i + 1 < len(terms) else terms[i] for i in range(0, len(terms), 2)
@@ -478,7 +495,7 @@
         unit = jnp.where(sub8 == 0, 1.0, 0.0)
         none = jnp.zeros((8, 128), jnp.float32)
         p_c, r_c, x_c = ([unit] + [none] * (PARTS - 1), [none, unit] + [none] * (PARTS - 2), [none] * PARTS)
-        norm = form(r_c, r_c)
+        norm = form(r_c, r_c, -1, 0)
         for step in range(S):
             q = [
                 diag_c[h] * p_c[h] + from_low[h] * pltpu.roll(p_c[h], 1, 0) + from_high[h] * pltpu.roll(p_c[h], 7, 0)
@@ -486,9 +503,9 @@
             ]
             if PARTS == 3:
                 q.append(jnp.where(sub8 == 0, 0.5 * HALF * splat(p_c[0], 7), 0.0))
-            length = norm / form(p_c, q)
+            length = norm / form(p_c, q, step + 1, step)
             r_next = [r_c[h] - length * q[h] for h in range(PARTS)]
-            norm_next = form(r_next, r_next)
+            norm_next = form(r_next, r_next, step + 1, min(step, S - 1))
             ratio = norm_next / norm
             new = (
                 [x_c[h] + length * p_c[h] for h in range(PARTS)] + r_next
@@ -550,7 +567,7 @@
                 pltpu.VMEM((S,) + field, f32),
                 pltpu.VMEM((S - 1,) + field, f32),
                 pltpu.VMEM(field, f32),
-                pltpu.VMEM((NZE, 24, 128), f32),
+                pltpu.VMEM((NZE, ROWS, 128), f32),
                 pltpu.VMEM((2, 2, BZ, 8, 128), f32),
                 pltpu.VMEM((2, BZ, 8, 128), f32),
                 pltpu.VMEM((PARTS, 8, 128), f32),

time: 94.6 us -> 92.5 us (0.978)
  Pallas kernels: 92.6 us -> 90.5 us
    pallas_call x1, Pallas kernels: 92.6 us -> 90.5 us  [local(): pl.pallas_call(kernel, out_shape=(jax.ShapeDtypeStruct(right_side.shape,...]
where the time goes in v7:
time: 92.5 us; the launch traced here: 92.4 us
  Pallas kernels  90.5 us (98%)
  local copies, waits for them, and re-layouts  1.26 us (1%)
    pallas_call x1, Pallas kernels, local(): pl.pallas_call(kernel, out_shape=(jax.ShapeDtypeStruct(right_side.shape,...  90.5 us

profile of v7, /device:TPU:1, one launch (start us, length us, event | category | flops | bytes accessed | tf_op | source)
XLA Modules:
  0.0 92.4 jit_solution(9638278245411220313)
XLA Ops:
  0.6 90.5 %shard_map.50 = (f32[8,16,128]{2,1,0:T(8,128)S(1)}, f32[8,16,128]{2,1,0:T(8,128)S(1)}) custom-call(f32[8,16,128]{2,1,0:T(8,128)} %rhs_ref.1, f32[8,16,128]{2,1,0:T(8,128)} %diag_ref.1, f32[17,3,8,128]{3,2,1,0:T(8,128)} %constant.2.clone.w_hbm), custom_call_target="tpu_custom_call" | custom-call | tf_op jit(solution)/shard_map/pallas_call | solution.py:560
  91.1 0.6 copy.7
  91.8 0.6 copy.8

commit v8 on v7

--- a/solution.py
+++ b/solution.py
@@ -91,10 +91,10 @@
         cp.start()
 
     plane = [
-        (((py + dy) % 4) * nzp + pz, (gy + dx) % 4, (gx + dc) % 2)
-        for dy in range(4) for dx in range(4) for dc in range(2) if dy or dx or dc
+        (((py + dy) % 4) * nzp + pz, (gy + dx) % 4, gx)
+        for dy in (2, 1, 3, 0) for dx in (2, 1, 3, 0) if dy or dx
     ]
-    line = [(py * nzp + (pz + dz) % nzp, gy, gx) for dz in range(1, nzp)]
+    line = [(py * nzp + (pz + dz) % nzp, gy, (gx + dc) % 2) for dz in (4, 3, 5, 2, 6, 1, 7, 0) for dc in range(2) if dz or dc]
     off_gy = gy + 2 * gx - 1
     has_off = (off_gy >= 0) & (off_gy < ny)
     to_z = (gz > 0, gz < nz - 1)
@@ -103,6 +103,9 @@
     barrier = pltpu.get_barrier_semaphore()
     for to in plane + line:
         pl.semaphore_signal(barrier, inc=1, device_id=to, device_id_type=MESH)
+    @pl.when(has_off)
+    def _():
+        pl.semaphore_signal(barrier, inc=1, device_id=(gz, off_gy, sib), device_id_type=MESH)
     for k, dz in enumerate((-1, 1)):
         @pl.when(to_z[k])
         def _(dz=dz):
@@ -137,7 +140,7 @@
         M[z] = row_in * jnp.where((at >= 0) & (at < nz * BZ), 1.0, 0.0)
 
     nz_near = jnp.where(gz > 0, 1, 0) + jnp.where(gz < nz - 1, 1, 0)
-    pl.semaphore_wait(barrier, len(plane) + len(line) + nz_near * jnp.where(has_off, 2, 1))
+    pl.semaphore_wait(barrier, len(plane) + len(line) + nz_near + jnp.where(has_off, nz_near + 1, 0))
     swaps = []
     for f in range(2):
         loads[f].wait()
@@ -160,18 +163,30 @@
         s1 = both + jnp.where(lane[:rows] == 127, 0.0, pltpu.roll(v[0], 127, 1))
         return s0, s1
 
-    def reorder(pair, order):
-        n = pair[0].shape[0]
-        wide = jnp.concatenate([pair[0].reshape(8 * n, 128), pair[1].reshape(8 * n, 128)], axis=1)
-        out = jnp.dot(wide, order, precision=lax.Precision.HIGHEST, preferred_element_type=jnp.float32)
-        return [out[:, 128 * h:128 * (h + 1)].reshape(n, 8, 128) for h in range(2)]
+    def reorder(pairs, order):
+        n = pairs[0][0].shape[0]
+        rows = 8 * n * len(pairs)
+        wide = jnp.concatenate(
+            [jnp.concatenate([v.reshape(8 * n, 128) for v in pair], axis=1) for pair in pairs], axis=0
+        )
+        high = wide.astype(jnp.bfloat16)
+        rest = wide - high.astype(jnp.float32)
+        mid = rest.astype(jnp.bfloat16)
+        low = (rest - mid.astype(jnp.float32)).astype(jnp.bfloat16)
+        out = jnp.dot(jnp.concatenate([high, mid, low], axis=0), order, preferred_element_type=jnp.float32)
+        out = out[:rows] + (out[rows:2 * rows] + out[2 * rows:])
+        return [
+            [out[8 * n * i:8 * n * (i + 1), 128 * h:128 * (h + 1)].reshape(n, 8, 128) for h in range(2)]
+            for i in range(len(pairs))
+        ]
 
     at_i = lax.broadcasted_iota(jnp.int32, (256, 256), 0)
     at_j = lax.broadcasted_iota(jnp.int32, (256, 256), 1)
-    to_stored = jnp.where(at_i == 2 * (at_j & 127) + (at_j >> 7), 1.0, 0.0)
-    to_natural = jnp.where(at_j == 2 * (at_i & 127) + (at_i >> 7), 1.0, 0.0)
-    for f in range(2):
-        halves = reorder(F[f, :, S:S + BZ, MID:MID + 8, :], to_stored)
+    to_stored = jnp.where(at_i == 2 * (at_j & 127) + (at_j >> 7), 1.0, 0.0).astype(jnp.bfloat16)
+    to_natural = jnp.where(at_j == 2 * (at_i & 127) + (at_i >> 7), 1.0, 0.0).astype(jnp.bfloat16)
+    for f, halves in enumerate(
+        reorder([[F[f, xt, S:S + BZ, MID:MID + 8, :] for xt in range(2)] for f in range(2)], to_stored)
+    ):
         for xt in range(2):
             F[f, xt, S:S + BZ, MID:MID + 8, :] = halves[xt]
 
@@ -202,6 +217,10 @@
     def forward(k, f):
         return remote(f, bands(k, f), bands(k, f), sib_rows, fs_sem.at[k, f], fr_sem.at[k, f], (gz, gy, sib))
 
+    def off_forward(k):
+        f = 1
+        return remote(f, bands(k, f), bands(k, f), off_rows, cs_sem.at[k, f], cr_sem.at[k, f], (gz, off_gy, sib))
+
     def y_off(f):
         return remote(f, own_z, own_z, off_rows, ys_sem.at[0, f], yr_sem.at[0, f], (gz, off_gy, sib))
 
@@ -212,7 +231,7 @@
         for k in range(2):
             @pl.when(to_z[k])
             def _(k=k):
-                for f in range(2):
+                for f in (1, 0):
                     z_copy(k, f).start()
 
         @pl.when(has_off)
@@ -222,17 +241,20 @@
         for k in range(2):
             @pl.when(to_z[k] & has_off)
             def _(k=k):
-                for f in range(2):
-                    corner(k, f).start()
+                corner(k, 0).start()
         for f in range(2):
             y_sib(f).start()
 
     def exchange_finish():
-        for f in range(2):
+        for f in (1, 0):
             for k in range(2):
                 @pl.when(from_z[k])
                 def _(k=k, f=f):
                     z_copy(k, f).wait_recv()
+                    if f == 1:
+                        @pl.when(has_off)
+                        def _():
+                            off_forward(k).start()
                     forward(k, f).start()
         for f in range(2):
             y_sib(f).wait_recv()
@@ -250,8 +272,8 @@
         for k in range(2):
             @pl.when(from_z[k] & has_off)
             def _(k=k):
-                for f in range(2):
-                    corner(k, f).wait_recv()
+                corner(k, 0).wait_recv()
+                off_forward(k).wait_recv()
 
     def exchange_sent():
         for f in range(2):
@@ -269,13 +291,16 @@
 
             @pl.when(to_z[k] & has_off)
             def _(k=k):
-                for f in range(2):
-                    corner(k, f).wait_send()
+                corner(k, 0).wait_send()
 
             @pl.when(from_z[k])
             def _(k=k):
                 for f in range(2):
                     forward(k, f).wait_send()
+
+            @pl.when(from_z[k] & has_off)
+            def _(k=k):
+                off_forward(k).wait_send()
 
     def power_steps(read, write, degree, z0, z1, rows):
         r0, n = rows
@@ -440,34 +465,35 @@
             picked = jnp.where(lane8 == k, jnp.sum(part, axis=1, keepdims=True), picked)
         local = jnp.sum(picked, axis=0, keepdims=True)
 
-        me1 = 8 * py + yv
+        me1 = 2 * pz + gx
+        me2 = 4 * py + gy
         @pl.when(t > 0)
         def _():
             exchange_sent()
         S1[par, me1] = local
-        for to in plane:
+        for to in line:
             pltpu.make_async_remote_copy(
                 src_ref=S1.at[par, me1], dst_ref=S1.at[par, me1],
                 send_sem=g1_s.at[par], recv_sem=g1_r.at[par],
                 device_id=to, device_id_type=MESH,
             ).start()
-        whole1 = pltpu.make_async_copy(S1.at[par, pl.ds(0, 31)], S1.at[par, pl.ds(0, 31)], g1_r.at[par])
+        whole1 = pltpu.make_async_copy(S1.at[par, pl.ds(0, 15)], S1.at[par, pl.ds(0, 15)], g1_r.at[par])
         whole1.wait()
-        S2[par, pz] = jnp.concatenate(exact_sum([(S1[par, i], None) for i in range(32)]), axis=0)
-        for to in line:
+        S2[par, me2] = jnp.concatenate(exact_sum([(S1[par, i], None) for i in range(16)]), axis=0)
+        for to in plane:
             pltpu.make_async_remote_copy(
-                src_ref=S2.at[par, pz], dst_ref=S2.at[par, pz],
+                src_ref=S2.at[par, me2], dst_ref=S2.at[par, me2],
                 send_sem=g2_s.at[par], recv_sem=g2_r.at[par],
                 device_id=to, device_id_type=MESH,
             ).start()
-        whole2 = pltpu.make_async_copy(S2.at[par, pl.ds(0, 7)], S2.at[par, pl.ds(0, 7)], g2_r.at[par])
+        whole2 = pltpu.make_async_copy(S2.at[par, pl.ds(0, 15)], S2.at[par, pl.ds(0, 15)], g2_r.at[par])
         whole2.wait()
-        high, low = exact_sum([(S2[par, i, 0:1], S2[par, i, 1:2]) for i in range(nzp)])
+        high, low = exact_sum([(S2[par, i, 0:1], S2[par, i, 1:2]) for i in range(16)])
         lead = high.astype(jnp.bfloat16).astype(jnp.float32)
         rest = (high - lead) + low
         lead, rest = jnp.broadcast_to(lead, (8, 128)), jnp.broadcast_to(rest, (8, 128))
-        pltpu.make_async_copy(S1.at[par, pl.ds(0, 31)], S1.at[par, pl.ds(0, 31)], g1_s.at[par]).wait()
-        pltpu.make_async_copy(S2.at[par, pl.ds(0, 7)], S2.at[par, pl.ds(0, 7)], g2_s.at[par]).wait()
+        pltpu.make_async_copy(S1.at[par, pl.ds(0, 15)], S1.at[par, pl.ds(0, 15)], g1_s.at[par]).wait()
+        pltpu.make_async_copy(S2.at[par, pl.ds(0, 15)], S2.at[par, pl.ds(0, 15)], g2_s.at[par]).wait()
 
         columns = 2 * S + 1
 
@@ -533,12 +559,12 @@
             device_id=(gz, gy, sib), device_id_type=MESH,
         )
 
-    halves = reorder(F[1, :, S:S + BZ, MID:MID + 8, :], to_natural)
+    (halves,) = reorder([[F[1, xt, S:S + BZ, MID:MID + 8, :] for xt in range(2)]], to_natural)
     for xt in range(2):
         F[1, xt, S:S + BZ, MID:MID + 8, :] = halves[xt]
     res_back = back(1, F.at[1, sib, own_z, own_rows, :])
     res_back.start()
-    halves = reorder([X[xt] + combine([XC[h] for h in range(PARTS)], xt) for xt in range(2)], to_natural)
+    (halves,) = reorder([[X[xt] + combine([XC[h] for h in range(PARTS)], xt) for xt in range(2)]], to_natural)
     for xt in range(2):
         X[xt] = halves[xt]
     sol_back = back(0, X.at[sib])
@@ -572,8 +598,8 @@
                 pltpu.VMEM((2, BZ, 8, 128), f32),
                 pltpu.VMEM((PARTS, 8, 128), f32),
                 pltpu.VMEM((2, BZ, 8, 128), f32),
-                pltpu.VMEM((2, 32, 1, 128), f32),
-                pltpu.VMEM((2, 8, 2, 128), f32),
+                pltpu.VMEM((2, 16, 1, 128), f32),
+                pltpu.VMEM((2, 16, 2, 128), f32),
                 pltpu.VMEM(table.shape, f32),
                 dma((5,)), dma((2, 2)), dma((2, 2)), dma((2, 2)), dma((2, 2)), dma((2, 2)), dma((2, 2)), dma((2, 2)), dma((2, 2)),
                 dma((4,)), dma((4,)), dma((2,)), dma((2,)), dma((2,)), dma((2,)),

time: 92.5 us -> 90.3 us (0.976)
  Pallas kernels: 90.5 us -> 88.3 us
    pallas_call x1, Pallas kernels: 90.5 us -> 88.3 us  [local(): pl.pallas_call(kernel, out_shape=(jax.ShapeDtypeStruct(right_side.shape,...]
where the time goes in v8:
time: 90.3 us; the launch traced here: 90.2 us
  Pallas kernels  88.3 us (98%)
  local copies, waits for them, and re-layouts  1.26 us (1%)
    pallas_call x1, Pallas kernels, local(): pl.pallas_call(kernel, out_shape=(jax.ShapeDtypeStruct(right_side.shape,...  88.3 us

profile of v8, /device:TPU:1, one launch (start us, length us, event | category | flops | bytes accessed | tf_op | source)
XLA Modules:
  0.0 90.2 jit_solution(5480819411009621853)
XLA Ops:
  0.6 88.3 %shard_map.50 = (f32[8,16,128]{2,1,0:T(8,128)S(1)}, f32[8,16,128]{2,1,0:T(8,128)S(1)}) custom-call(f32[8,16,128]{2,1,0:T(8,128)} %rhs_ref.1, f32[8,16,128]{2,1,0:T(8,128)} %diag_ref.1, f32[17,3,8,128]{3,2,1,0:T(8,128)} %constant.2.clone.w_hbm), custom_call_target="tpu_custom_call" | custom-call | tf_op jit(solution)/shard_map/pallas_call | solution.py:586
  88.9 0.6 copy.7
  89.6 0.6 copy.8

commit v9 on v8

--- a/solution.py
+++ b/solution.py
@@ -227,23 +227,21 @@
     def y_sib(f):
         return remote(f, own_z, own_z, sib_rows, ys_sem.at[1, f], yr_sem.at[1, f], (gz, gy, sib))
 
-    def exchange_start():
+    def exchange_start(f):
         for k in range(2):
             @pl.when(to_z[k])
             def _(k=k):
-                for f in (1, 0):
-                    z_copy(k, f).start()
+                z_copy(k, f).start()
 
         @pl.when(has_off)
         def _():
-            for f in range(2):
-                y_off(f).start()
-        for k in range(2):
-            @pl.when(to_z[k] & has_off)
-            def _(k=k):
-                corner(k, 0).start()
-        for f in range(2):
-            y_sib(f).start()
+            y_off(f).start()
+        if f == 0:
+            for k in range(2):
+                @pl.when(to_z[k] & has_off)
+                def _(k=k):
+                    corner(k, 0).start()
+        y_sib(f).start()
 
     def exchange_finish():
         for f in (1, 0):
@@ -396,8 +394,6 @@
 
     def outer(t, carry):
         par = t % 2
-        exchange_start()
-
         @pl.when(t > 0)
         def _():
             for xt in range(2):
@@ -544,12 +540,20 @@
             x_c, r_c, p_c, norm = new[:PARTS], new[PARTS:2 * PARTS], new[2 * PARTS:3 * PARTS], new[-1]
 
         for xt in range(2):
-            F[0, xt, S:S + BZ, MID:MID + 8, :] = combine(p_c, xt)
             F[1, xt, S:S + BZ, MID:MID + 8, :] = combine(r_c, xt)
+
+        @pl.when(t < len(INNER) - 1)
+        def _():
+            exchange_start(1)
+            for xt in range(2):
+                F[0, xt, S:S + BZ, MID:MID + 8, :] = combine(p_c, xt)
+            exchange_start(0)
         for h in range(PARTS):
             XC[h] = x_c[h]
         return carry
 
+    exchange_start(1)
+    exchange_start(0)
     lax.fori_loop(0, len(INNER), outer, 0)
 
     def back(f, src):

time: 90.3 us -> 89.9 us (level)
  no operation moved by 1% of the time
where the time goes in v9:
time: 89.9 us; the launch traced here: 89.8 us
  Pallas kernels  87.9 us (98%)
  local copies, waits for them, and re-layouts  1.26 us (1%)
    pallas_call x1, Pallas kernels, local(): pl.pallas_call(kernel, out_shape=(jax.ShapeDtypeStruct(right_side.shape,...  87.9 us

profile of v9, /device:TPU:1, one launch (start us, length us, event | category | flops | bytes accessed | tf_op | source)
XLA Modules:
  0.0 89.8 jit_solution(15332030868798376047)
XLA Ops:
  0.6 87.9 %shard_map.50 = (f32[8,16,128]{2,1,0:T(8,128)S(1)}, f32[8,16,128]{2,1,0:T(8,128)S(1)}) custom-call(f32[8,16,128]{2,1,0:T(8,128)} %rhs_ref.1, f32[8,16,128]{2,1,0:T(8,128)} %diag_ref.1, f32[17,3,8,128]{3,2,1,0:T(8,128)} %constant.2.clone.w_hbm), custom_call_target="tpu_custom_call" | custom-call | tf_op jit(solution)/shard_map/pallas_call | solution.py:590
  88.6 0.6 copy.7
  89.2 0.6 copy.8

commit v10 on v9

--- a/solution.py
+++ b/solution.py
@@ -419,22 +419,29 @@
         def late_rows(core, m):
             return (MID + m if core else MID - m, 8)
 
-        def powers(rows, core):
+        def powers(rows, core, fields=(0, 1)):
             for degree in range(1, S + 1):
-                for f, (read, write) in enumerate(((read_p, write_p), (read_r, write_r))):
+                for f in fields:
+                    read, write = ((read_p, write_p), (read_r, write_r))[f]
                     m = S - f - degree
                     if m >= 0 and rows(core, m)[1]:
                         power_steps(read, write, degree, degree + f, NZE - degree - f, rows(core, m))
 
         for core in range(2):
-            @pl.when(gx == core)
+            @pl.when((gx == core) & (t > 0))
             def _(core=core):
                 powers(early_rows, core)
-
-                @pl.when(t > 0)
-                def _():
-                    exchange_last()
+                exchange_last()
                 powers(late_rows, core)
+
+        @pl.when(t == 0)
+        def _():
+            for degree in range(1, S + 1):
+                m = S - degree
+                rows = (LO, 24) if m > 4 else (MID - 4, 16) if m else (MID, 8)
+                power_steps(read_p, write_p, degree, degree, NZE - degree, rows)
+            for degree in range(1, S):
+                RV[degree - 1, :, S:S + BZ, MID:MID + 8, :] = PV[degree - 1, :, S:S + BZ, MID:MID + 8, :]
 
         parts = [None] * (NPP + NPR + NRR)
 

time: 89.9 us -> 89.1 us (level)
  no operation moved by 1% of the time
where the time goes in v10:
time: 89.1 us
  Pallas kernels  87.2 us (98%)
  local copies, waits for them, and re-layouts  1.26 us (1%)
    pallas_call x1, Pallas kernels, local(): pl.pallas_call(kernel, out_shape=(jax.ShapeDtypeStruct(right_side.shape,...  87.2 us

profile of v10, /device:TPU:1, one launch (start us, length us, event | category | flops | bytes accessed | tf_op | source)
XLA Modules:
  0.0 89.1 jit_solution(6618056636202755814)
XLA Ops:
  0.6 87.2 %shard_map.50 = (f32[8,16,128]{2,1,0:T(8,128)S(1)}, f32[8,16,128]{2,1,0:T(8,128)S(1)}) custom-call(f32[8,16,128]{2,1,0:T(8,128)} %rhs_ref.1, f32[8,16,128]{2,1,0:T(8,128)} %diag_ref.1, f32[17,3,8,128]{3,2,1,0:T(8,128)} %constant.2.clone.w_hbm), custom_call_target="tpu_custom_call" | custom-call | tf_op jit(solution)/shard_map/pallas_call | solution.py:597
  87.8 0.6 copy.7
  88.4 0.6 copy.8

commit v11 on v10

--- a/solution.py
+++ b/solution.py
@@ -192,7 +192,8 @@
 
     off_rows = pl.ds(pl.multiple_of(LO + 16 * sib, 8), 8)
     sib_rows = pl.ds(pl.multiple_of(LO + 16 * gx, 8), 8)
-    near = (gz - 1, gz + 1)
+    near = (jnp.maximum(gz - 1, 0), jnp.minimum(gz + 1, nz - 1))
+    beyond = jnp.clip(off_gy, 0, ny - 1)
 
     def bands(k, f):
         return (pl.ds(S + BZ, S - f), pl.ds(f, S - f))[k]
@@ -211,7 +212,7 @@
 
     def corner(k, f):
         return remote(
-            f, edges(k, f), bands(k, f), off_rows, cs_sem.at[k, f], cr_sem.at[k, f], (near[k], off_gy, sib)
+            f, edges(k, f), bands(k, f), off_rows, cs_sem.at[k, f], cr_sem.at[k, f], (near[k], beyond, sib)
         )
 
     def forward(k, f):
@@ -219,10 +220,10 @@
 
     def off_forward(k):
         f = 1
-        return remote(f, bands(k, f), bands(k, f), off_rows, cs_sem.at[k, f], cr_sem.at[k, f], (gz, off_gy, sib))
+        return remote(f, bands(k, f), bands(k, f), off_rows, cs_sem.at[k, f], cr_sem.at[k, f], (gz, beyond, sib))
 
     def y_off(f):
-        return remote(f, own_z, own_z, off_rows, ys_sem.at[0, f], yr_sem.at[0, f], (gz, off_gy, sib))
+        return remote(f, own_z, own_z, off_rows, ys_sem.at[0, f], yr_sem.at[0, f], (gz, beyond, sib))
 
     def y_sib(f):
         return remote(f, own_z, own_z, sib_rows, ys_sem.at[1, f], yr_sem.at[1, f], (gz, gy, sib))

time: 89.1 us -> 89.1 us (level)
  no operation moved by 1% of the time
where the time goes in v11:
time: 89.1 us
  Pallas kernels  87.2 us (98%)
  local copies, waits for them, and re-layouts  1.26 us (1%)
    pallas_call x1, Pallas kernels, local(): pl.pallas_call(kernel, out_shape=(jax.ShapeDtypeStruct(right_side.shape,...  87.2 us

profile of v11, /device:TPU:1, one launch (start us, length us, event | category | flops | bytes accessed | tf_op | source)
XLA Modules:
  0.0 89.1 jit_solution(4868649453288106791)
XLA Ops:
  0.6 87.2 %shard_map.50 = (f32[8,16,128]{2,1,0:T(8,128)S(1)}, f32[8,16,128]{2,1,0:T(8,128)S(1)}) custom-call(f32[8,16,128]{2,1,0:T(8,128)} %rhs_ref.1, f32[8,16,128]{2,1,0:T(8,128)} %diag_ref.1, f32[17,3,8,128]{3,2,1,0:T(8,128)} %constant.2.clone.w_hbm), custom_call_target="tpu_custom_call" | custom-call | tf_op jit(solution)/shard_map/pallas_call | solution.py:598
  87.8 0.6 copy.7
  88.4 0.6 copy.8
